TPU v7x, 128 devices: a whole 4x4x4 slice. The times are simulated.
128 devices in a mesh: ep: 8 (over y, core), fs: 16 (over z, x).
Axes of the slice: x: 4, y: 4, z: 4, core: 2. Of those that a mesh axis runs over, the one named last changes fastest.
Arguments:
- grads: bfloat16 [8, 8, 256, 14336], P('ep', None, 'fs'), may hold values from -64 to 64
- counts: int32 [8, 8], replicated, may hold values from 16 to 2047
- weight: bfloat16 [8, 256, 14336], P('ep', 'fs'), may hold values from -3 to 3
- mom: float32 [8, 256, 14336], P('ep', 'fs'), may hold values from -64 to 64
- second: float32 [8, 256, 14336], P('ep', 'fs'), may hold values from 0.1 to 10
- in_weight: float32 [6, 32], replicated, may hold values from -2.5 to 2.5
- in_bias: float32 [32], replicated, may hold values from -3 to 3
- out_weight: float32 [32, 2], replicated, may hold values from -1 to 1
- out_bias: float32 [2], replicated, may hold values from -3 to 3
Outputs:
- new_weight: bfloat16 [8, 256, 14336], P('ep')
- new_mom: float32 [8, 256, 14336], P('ep', 'fs')
- new_second: float32 [8, 256, 14336], P('ep', 'fs')
All inputs are finite; a program needn't handle non-finite values.
Results may differ from a plain program's by a relative error of at most 0.0019.
Values may be sent and summed in bfloat16 or wider, within the bound.
A program may use at most 64 MiB of HBM per device.

v0:
```python
import functools

import jax
import jax.numpy as jnp
from jax import lax
from jax.experimental import pallas as pl
from jax.experimental.pallas import tpu as pltpu
from jax.sharding import PartitionSpec as P

MOMENTUM_DECAY = 0.9
SECOND_DECAY = 0.99
NORM_EPS = 1e-06
ROOT_EPS = 1e-08
STEP_SCALE = 0.2
EXP_SCALE = 0.5
LANES = 128
MOST_CHUNKS = 14
MOST_CUTS = 4
LAG = 3
VMEM_BYTES = 67043328


def largest_divisor(number, most):
    return max(d for d in range(1, most + 1) if number % d == 0)


def tile_width(columns, most):
    return LANES * largest_divisor(columns // LANES, most // LANES)


def turned_chunks(depth, across, chunks):
    def load(turned):
        straight = chunks - turned
        on_x = (across - 1) * (depth * straight + turned)
        on_z = (depth - 1) * (straight + across * turned)
        return max(on_x, on_z)

    return min(range(chunks + 1), key=load)


def remote(src, dst, send_sem, recv_sem, axis, peer):
    return pltpu.make_async_remote_copy(
        src_ref=src,
        dst_ref=dst,
        send_sem=send_sem,
        recv_sem=recv_sem,
        device_id={axis: peer},
        device_id_type=pl.DeviceIdType.MESH,
    )


def kernel(
    groups,
    depth,
    across,
    chunks,
    counts_hbm,
    in_weight_hbm,
    in_bias_hbm,
    out_weight_hbm,
    out_bias_hbm,
    grads_hbm,
    weight_hbm,
    mom_hbm,
    second_hbm,
    gathered_hbm,
    mom_hbm_out,
    second_hbm_out,
    counts,
    in_weight,
    in_bias,
    out_weight,
    out_bias,
    grads,
    weight,
    mom,
    second,
    gathered,
    outgoing,
    arrived,
    gradient,
    sums,
    bias,
    small_sem,
    slab_sem,
    param_sem,
    grad_send,
    grad_recv,
    flush_sem,
    state_sem,
    sum_send,
    sum_recv,
    row_send,
    row_recv,
):
    shards = depth * across
    rows, columns = mom.shape
    units = in_bias.shape[0]
    me_group = lax.axis_index("ep")
    me = lax.axis_index("fs")
    z = me // across
    x = me % across

    def peer_of(step):
        return (me_group + step) % groups

    small = [
        pltpu.make_async_copy(src, dst, small_sem.at[i])
        for i, (src, dst) in enumerate(
            (
                (counts_hbm, counts),
                (in_weight_hbm, in_weight),
                (in_bias_hbm, in_bias),
                (out_weight_hbm, out_weight),
                (out_bias_hbm, out_bias),
            )
        )
    ]
    for copy in small:
        copy.start()

    slabs = [
        pltpu.make_async_copy(
            grads_hbm.at[0, peer_of(step)], grads.at[step], slab_sem.at[step]
        )
        for step in range(groups)
    ]
    for copy in slabs[1:] + slabs[:1]:
        copy.start()
    params = [
        pltpu.make_async_copy(src.at[0], dst, param_sem.at[i])
        for i, (src, dst) in enumerate(
            (
                (mom_hbm, mom),
                (second_hbm, second),
                (weight_hbm, weight),
            )
        )
    ]
    for copy in params:
        copy.start()

    barrier = pltpu.get_barrier_semaphore()
    for step in range(1, groups):
        pl.semaphore_signal(
            barrier,
            inc=1,
            device_id={"ep": peer_of(step)},
            device_id_type=pl.DeviceIdType.MESH,
        )
    for step in range(1, shards):
        pl.semaphore_signal(
            barrier,
            inc=1,
            device_id={"fs": (me + step) % shards},
            device_id_type=pl.DeviceIdType.MESH,
        )
    pl.semaphore_wait(barrier, groups - 1 + shards - 1)
    for copy in small:
        copy.wait()

    cuts = grad_recv.shape[1]
    cut = columns // cuts
    narrow = tile_width(cut, 512)

    def cols_of(c, i):
        return pl.ds(pl.multiple_of(c * cut + i * narrow, narrow), narrow)

    def piece_of(c):
        return pl.ds(pl.multiple_of(c * cut, cut), cut)

    def share_of(expert):
        total = counts[0, expert]
        for s in range(1, groups):
            total = total + counts[s, expert]
        mine = jnp.full((1, LANES), counts[me_group, expert].astype(jnp.float32))
        return (mine / jnp.full((1, LANES), total.astype(jnp.float32)))[:, :1]

    shares = [share_of(peer_of(step)) for step in range(groups)]

    def weighted(step, cols):
        value = shares[step] * grads[step, :, cols].astype(jnp.float32)
        return value.astype(jnp.bfloat16)

    def grad_copy(step, c):
        return remote(
            outgoing.at[step - 1, :, piece_of(c)],
            arrived.at[step - 1, :, piece_of(c)],
            grad_send.at[step - 1, c],
            grad_recv.at[step - 1, c],
            "ep",
            peer_of(step),
        )

    order = sorted(range(1, groups), key=lambda step: abs(2 * step - groups))
    for copy in slabs:
        copy.wait()

    def send_piece(c, carry):
        for step in order:

            def weigh(i, inner, step=step):
                cols = cols_of(c, i)
                outgoing[step - 1, :, cols] = weighted(step, cols)
                return inner

            lax.fori_loop(0, cut // narrow, weigh, 0)
            grad_copy(step, c).start()
        return carry

    lax.fori_loop(0, cuts, send_piece, 0)
    for copy in params:
        copy.wait()


    def moments(c, carry):
        for step in range(1, groups):
            grad_copy(step, c).wait_recv()

        def one(i, inner):
            grad_acc, mom_acc = inner
            cols = cols_of(c, i)
            total = weighted(0, cols).astype(jnp.float32)
            for step in range(1, groups):
                total = total + arrived[step - 1, :, cols].astype(jnp.float32)
            mom_next = MOMENTUM_DECAY * mom[:, cols] + (1.0 - MOMENTUM_DECAY) * total
            gradient[:, cols] = total
            mom[:, cols] = mom_next
            second[:, cols] = (
                SECOND_DECAY * second[:, cols] + (1.0 - SECOND_DECAY) * total * total
            )
            return grad_acc + total * total, mom_acc + mom_next * mom_next

        return lax.fori_loop(0, cut // narrow, one, carry)

    zero = jnp.zeros((rows, narrow), jnp.float32)
    grad_acc, mom_acc = lax.fori_loop(0, cuts, moments, (zero, zero))

    def to_lanes(acc):
        acc = jnp.sum(acc, axis=0, keepdims=True)
        return sum(acc[:, j : j + LANES] for j in range(0, narrow, LANES))

    sums[me, 0:1, :] = to_lanes(grad_acc)
    sums[me, 1:2, :] = to_lanes(mom_acc)
    sum_sends = []
    for step in range(1, shards):
        copy = remote(
            sums.at[me],
            sums.at[me],
            sum_send.at[step - 1],
            sum_recv.at[me],
            "fs",
            (me + step) % shards,
        )
        copy.start()
        sum_sends.append(copy)
    for step in range(1, shards):
        source = (me + step) % shards
        remote(
            sums.at[source],
            sums.at[source],
            sum_send.at[step - 1],
            sum_recv.at[source],
            "fs",
            source,
        ).wait_recv()

    states = [
        pltpu.make_async_copy(mom, mom_hbm_out.at[0], state_sem.at[0]),
        pltpu.make_async_copy(second, second_hbm_out.at[0], state_sem.at[1]),
    ]
    for copy in states:
        copy.start()

    entries = rows * columns * shards
    totals = sums[0]
    for s in range(1, shards):
        totals = totals + sums[s]
    mean = jnp.broadcast_to(jnp.sum(totals, axis=1, keepdims=True) / entries, (2, LANES)) + NORM_EPS
    inverse = lax.rsqrt(mean)
    inv_grad = inverse[0:1, :1]
    inv_mom = inverse[1:2, :1]
    log_mom = jnp.max(0.5 * jnp.log(mean[1:2, :]))
    for h in range(units):
        bias[h] = in_bias[h] + in_weight[5, h] * log_mom

    width = columns // chunks
    tile = tile_width(width, 256)

    def learned_step(cols):
        grad = gradient[:, cols]
        mom_next = mom[:, cols]
        old = weight[:, cols].astype(jnp.float32)
        inv_root = lax.rsqrt(second[:, cols] + ROOT_EPS)
        features = (
            grad * inv_grad,
            mom_next * inv_mom,
            mom_next * inv_root,
            grad * inv_root,
            old,
        )
        direction = jnp.full(grad.shape, out_bias[0])
        magnitude = jnp.full(grad.shape, out_bias[1])
        for h in range(units):
            hidden = features[0] * in_weight[0, h] + bias[h]
            for f in range(1, len(features)):
                hidden = hidden + features[f] * in_weight[f, h]
            hidden = jnp.maximum(hidden, 0.0)
            direction = direction + hidden * out_weight[0, h]
            magnitude = magnitude + hidden * out_weight[1, h]
        update = STEP_SCALE * direction * jnp.exp(EXP_SCALE * magnitude)
        return (old - update).astype(jnp.bfloat16)

    def rows_of(source):
        return pl.ds(pl.multiple_of(source * rows, rows), rows)

    ways = (
        (across, z < depth - 1),
        (-across, z > 0),
        (1, x < across - 1),
        (-1, x > 0),
    )
    turned = turned_chunks(depth, across, chunks)
    along_z = (z, depth, across, (0, 1))
    along_x = (x, across, 1, (2, 3))
    trees = ((along_x, along_z, 0, turned), (along_z, along_x, turned, chunks))

    def block(source, k):
        return gathered.at[rows_of(source), pl.ds(pl.multiple_of(k * width, width), width)]

    def send(tree, source, k, which):
        for number in which:
            offset, possible = ways[number]

            @pl.when(possible)
            def _(number=number, offset=offset):
                piece = block(source, k)
                remote(
                    piece,
                    piece,
                    row_send.at[tree, number, source],
                    row_recv.at[source, k],
                    "fs",
                    me + offset,
                ).start()

    def flush(source, k):
        cols = pl.ds(pl.multiple_of(k * width, width), width)
        pltpu.make_async_copy(
            block(source, k), gathered_hbm.at[0, rows_of(source), cols], flush_sem.at[source]
        ).start()

    def await_block(source, k):
        piece = block(source, k)
        remote(
            piece, piece, row_send.at[0, 0, source], row_recv.at[source, k], "fs", source
        ).wait_recv()

    def relay(t, tree):
        first, second, low, high = trees[tree]
        if low == high:
            return
        at, size, stride, (up, down) = first
        for d in range(1, size):
            k = t - LAG * d
            live = jnp.logical_and(k >= low, k < high)

            @pl.when(jnp.logical_and(live, at >= d))
            def _(d=d, k=k):
                source = me - d * stride
                await_block(source, k)
                send(tree, source, k, (up,) + second[3])
                flush(source, k)

            @pl.when(jnp.logical_and(live, at + d < size))
            def _(d=d, k=k):
                source = me + d * stride
                await_block(source, k)
                send(tree, source, k, (down,) + second[3])
                flush(source, k)

        other, length, pitch, (up_other, down_other) = second
        for e in range(1, length):
            k = t - LAG * (size - 1 + e)
            live = jnp.logical_and(k >= low, k < high)
            for level in range(size):

                @pl.when(jnp.logical_and(live, other >= e))
                def _(e=e, k=k, level=level):
                    source = level * stride + (other - e) * pitch
                    await_block(source, k)
                    send(tree, source, k, (up_other,))
                    flush(source, k)

                @pl.when(jnp.logical_and(live, other + e < length))
                def _(e=e, k=k, level=level):
                    source = level * stride + (other + e) * pitch
                    await_block(source, k)
                    send(tree, source, k, (down_other,))
                    flush(source, k)

    def turn(t, carry):
        @pl.when(t < chunks)
        def _():
            def one(i, inner):
                cols = pl.ds(pl.multiple_of(t * width + i * tile, tile), tile)
                gathered[rows_of(me), cols] = learned_step(cols)
                return inner

            lax.fori_loop(0, width // tile, one, 0)

        for tree in range(2):
            _, _, low, high = trees[tree]

            @pl.when(jnp.logical_and(t >= low, t < high))
            def _(tree=tree):
                send(tree, me, t, (0, 1, 2, 3))
                flush(me, t)

        for tree in range(2):
            relay(t, tree)
        return carry

    lax.fori_loop(0, chunks + LAG * (depth - 1 + across - 1), turn, 0)

    def drain(c, carry):
        for step in range(1, groups):
            grad_copy(step, c).wait_send()
        return carry

    lax.fori_loop(0, cuts, drain, 0)
    for copy in sum_sends:
        copy.wait_send()
    for copy in states:
        copy.wait()
    for source in range(shards):
        pltpu.make_async_copy(
            gathered.at[rows_of(source), :],
            gathered_hbm.at[0, rows_of(source), :],
            flush_sem.at[source],
        ).wait()
    for tree in range(2):
        first, _, low, high = trees[tree]
        if low == high:
            continue
        for number, (_, possible) in enumerate(ways):
            for source in range(shards):
                level, place = source // across, source % across
                used = (level <= z, level >= z, place <= x, place >= x)[number]
                if first is along_z and number < 2:
                    used = jnp.logical_and(used, place == x)
                if first is along_x and number >= 2:
                    used = jnp.logical_and(used, level == z)

                @pl.when(jnp.logical_and(possible, used))
                def _(tree=tree, number=number, source=source, low=low, high=high):
                    piece = gathered.at[rows_of(source), pl.ds(low * width, (high - low) * width)]
                    remote(
                        piece,
                        piece,
                        row_send.at[tree, number, source],
                        row_recv.at[source, low],
                        "fs",
                        (me + 1) % shards,
                    ).wait_send()


def per_device(
    groups, shards, grads, counts, weight, mom, second, in_weight, in_bias, out_weight, out_bias
):
    rows, columns = mom.shape[1], mom.shape[2]
    across = max(d for d in range(1, shards + 1) if shards % d == 0 and d * d <= shards)
    depth = shards // across
    chunks = largest_divisor(columns // LANES, MOST_CHUNKS)
    cuts = largest_divisor(columns // LANES, MOST_CUTS)
    hbm = pl.BlockSpec(memory_space=pltpu.HBM)
    return pl.pallas_call(
        functools.partial(kernel, groups, depth, across, chunks),
        out_shape=(
            jax.ShapeDtypeStruct((1, rows * shards, columns), jnp.bfloat16),
            jax.ShapeDtypeStruct(mom.shape, jnp.float32),
            jax.ShapeDtypeStruct(second.shape, jnp.float32),
        ),
        in_specs=[hbm] * 9,
        out_specs=(hbm, hbm, hbm),
        scratch_shapes=[
            pltpu.SMEM(counts.shape, jnp.int32),
            pltpu.SMEM(in_weight.shape, jnp.float32),
            pltpu.SMEM(in_bias.shape, jnp.float32),
            pltpu.SMEM(out_weight.shape[::-1], jnp.float32),
            pltpu.SMEM(out_bias.shape, jnp.float32),
            pltpu.VMEM((groups, rows, columns), jnp.bfloat16),
            pltpu.VMEM((rows, columns), jnp.bfloat16),
            pltpu.VMEM((rows, columns), jnp.float32),
            pltpu.VMEM((rows, columns), jnp.float32),
            pltpu.VMEM((rows * shards, columns), jnp.bfloat16),
            pltpu.VMEM((groups - 1, rows, columns), jnp.bfloat16),
            pltpu.VMEM((groups - 1, rows, columns), jnp.bfloat16),
            pltpu.VMEM((rows, columns), jnp.float32),
            pltpu.VMEM((shards, 2, LANES), jnp.float32),
            pltpu.SMEM((in_bias.shape[0],), jnp.float32),
            pltpu.SemaphoreType.DMA((5,)),
            pltpu.SemaphoreType.DMA((groups,)),
            pltpu.SemaphoreType.DMA((3,)),
            pltpu.SemaphoreType.DMA((groups - 1, cuts)),
            pltpu.SemaphoreType.DMA((groups - 1, cuts)),
            pltpu.SemaphoreType.DMA((shards,)),
            pltpu.SemaphoreType.DMA((2,)),
            pltpu.SemaphoreType.DMA((shards - 1,)),
            pltpu.SemaphoreType.DMA((shards,)),
            pltpu.SemaphoreType.DMA((2, 4, shards)),
            pltpu.SemaphoreType.DMA((shards, chunks)),
        ],
        compiler_params=pltpu.CompilerParams(
            collective_id=0, has_side_effects=True, vmem_limit_bytes=VMEM_BYTES
        ),
        name="learned_update",
    )(counts, in_weight, in_bias, out_weight.T, out_bias, grads, weight, mom, second)


def solution(mesh):
    in_specs = (
        P("ep", None, "fs", None),
        P(),
        P("ep", "fs", None),
        P("ep", "fs", None),
        P("ep", "fs", None),
        P(),
        P(),
        P(),
        P(),
    )
    out_specs = (P("ep", None, None), P("ep", "fs", None), P("ep", "fs", None))
    body = functools.partial(per_device, mesh.shape["ep"], mesh.shape["fs"])
    return jax.shard_map(
        body, mesh=mesh, in_specs=in_specs, out_specs=out_specs, check_vma=False
    )
```

profile of v0, /device:TPU:0, one launch (start us, length us, event | category | flops | bytes accessed | tf_op | source)
XLA Modules:
  0.0 174.8 jit_solution(11713218427441056047)
XLA Ops:
  0.6 165.2 %learned_update.1 = (bf16[1,256,14336]{2,1,0:T(8,128)(2,1)}, f32[1,16,14336]{2,1,0:T(8,128)}, f32[1,16,14336]{2,1,0:T(8,128)}) custom-call(s32[8,8]{1,0:T(8,128)} %counts_hbm.1, f32[6,32]{1,0:T(8,128)} %in_weight_hbm.1, f32[32]{0:T(128)} %in_bias_hbm.1, f32[2,32]{1,0:T(2,128)} %bitcast.1, f32[2]{0:T(128)} %out_bias_hbm.1, ...), custom_call_target="tpu_custom_call" | custom-call | tf_op jit(solution)/shard_map/learned_update/pallas_call | solution.py:477
  165.9 0.0 copy-start.1
  165.9 0.0 copy-start
  165.9 7.0 %copy.15 = bf16[1,256,14336]{2,1,0:T(8,128)(2,1)} copy(bf16[1,256,14336]{2,1,0:T(8,128)(2,1)} %get-tuple-element.6) | data formatting | bytes 14680064
  172.9 0.0 copy-done.1
  172.9 0.9 copy.16
  173.8 0.0 copy-done
  173.8 0.9 copy.17
Async XLA Ops:
  165.9 7.1 %copy-start.1 = (f32[1,16,14336]{2,1,0:T(8,128)S(1)}, f32[1,16,14336]{2,1,0:T(8,128)}, u32[]{:S(2)}) copy-start(f32[1,16,14336]{2,1,0:T(8,128)} %get-tuple-element.7) | copy-start | bytes 2752516
  165.9 8.0 %copy-start = (f32[1,16,14336]{2,1,0:T(8,128)S(1)}, f32[1,16,14336]{2,1,0:T(8,128)}, u32[]{:S(2)}) copy-start(f32[1,16,14336]{2,1,0:T(8,128)} %get-tuple-element.8) | copy-start | bytes 2752516
where the time goes:
time: 175 us
  Pallas kernels  165 us (94%)
  local copies, waits for them, and re-layouts  8.88 us (5%)
    pallas_call x1, Pallas kernels, per_device(): pl.pallas_call(functools.partial(kernel, groups, depth, across, chunks),...  165 us
    unnamed x7, local copies, waits for them, and re-layouts  8.88 us

commit v1 on v0

v1 whole, which is shorter than its diff:
```python
import functools

import jax
import jax.numpy as jnp
from jax import lax
from jax.experimental import pallas as pl
from jax.experimental.pallas import tpu as pltpu
from jax.sharding import PartitionSpec as P

MOMENTUM_DECAY = 0.9
SECOND_DECAY = 0.99
NORM_EPS = 1e-06
ROOT_EPS = 1e-08
STEP_SCALE = 0.2
EXP_SCALE = 0.5
LANES = 128
CORES = 2
SIDE = 4
CHUNKS = 16
PIECES = 7
LAG_ONE = 3
LAG_TWO = 6
LAG_THREE = 9
GATE_PIECE = 5
VMEM_BYTES = 67043328 - 9175040


def largest_divisor(number, most):
    return max(d for d in range(1, most + 1) if number % d == 0)


def tile_width(columns, most):
    return LANES * largest_divisor(columns // LANES, most // LANES)


def remote(src, dst, send_sem, recv_sem, axis, peer):
    return pltpu.make_async_remote_copy(
        src_ref=src,
        dst_ref=dst,
        send_sem=send_sem,
        recv_sem=recv_sem,
        device_id={axis: peer},
        device_id_type=pl.DeviceIdType.MESH,
    )


def kernel(
    ring,
    counts_hbm,
    in_weight_hbm,
    in_bias_hbm,
    out_weight_hbm,
    out_bias_hbm,
    grads_hbm,
    weight_hbm,
    mom_hbm,
    second_hbm,
    gathered_out,
    mom_out,
    second_out,
    counts,
    in_weight,
    in_bias,
    out_weight,
    out_bias,
    grads,
    weight,
    pair_out,
    pair_in,
    ring_out,
    ring_in,
    gradient,
    sums,
    bias,
    small_sem,
    slab_sem,
    param_sem,
    pair_send,
    pair_recv,
    ring_send,
    ring_recv,
    gate,
    sum_send,
    sum_recv,
    row_send,
    pass_recv,
    last_recv,
):
    gathered = gathered_out.at[0]
    mom = mom_out.at[0]
    second = second_out.at[0]
    groups = ring * CORES
    shards = SIDE * SIDE
    rows, columns = gradient.shape
    units = in_bias.shape[0]
    me_group = lax.axis_index("ep")
    me = lax.axis_index("fs")
    y = me_group // CORES
    core = me_group % CORES
    partner = y * CORES + 1 - core
    z = me // SIDE
    x = me % SIDE

    def group_of(step, which):
        return (y + step) % ring * CORES + which

    small = [
        pltpu.make_async_copy(src, dst, small_sem.at[i])
        for i, (src, dst) in enumerate(
            (
                (counts_hbm, counts),
                (in_weight_hbm, in_weight),
                (in_bias_hbm, in_bias),
                (out_weight_hbm, out_weight),
                (out_bias_hbm, out_bias),
            )
        )
    ]
    for copy in small:
        copy.start()

    def slab(which, step):
        return pltpu.make_async_copy(
            grads_hbm.at[0, group_of(step, which)],
            grads.at[which, step],
            slab_sem.at[which, step],
        )

    for which in range(CORES):
        for step in range(ring):
            slab(which, step).start()
    params = [
        pltpu.make_async_copy(src.at[0], dst, param_sem.at[i])
        for i, (src, dst) in enumerate(
            ((mom_hbm, mom), (second_hbm, second), (weight_hbm, weight))
        )
    ]
    for copy in params:
        copy.start()

    barrier = pltpu.get_barrier_semaphore()
    for peer in [partner] + [group_of(step, core) for step in range(1, ring)]:
        pl.semaphore_signal(
            barrier, inc=1, device_id={"ep": peer}, device_id_type=pl.DeviceIdType.MESH
        )
    for step in range(1, shards):
        pl.semaphore_signal(
            barrier,
            inc=1,
            device_id={"fs": (me + step) % shards},
            device_id_type=pl.DeviceIdType.MESH,
        )
    for copy in small:
        copy.wait()

    pieces = ring_recv.shape[1]
    piece = columns // pieces
    narrow = tile_width(piece, 512)

    def cols_of(p, i):
        return pl.ds(pl.multiple_of(p * piece + i * narrow, narrow), narrow)

    def piece_of(p):
        return pl.ds(pl.multiple_of(p * piece, piece), piece)

    def share_of(expert):
        total = counts[0, expert]
        for s in range(1, groups):
            total = total + counts[s, expert]
        mine = jnp.full((1, LANES), counts[me_group, expert].astype(jnp.float32))
        return (mine / jnp.full((1, LANES), total.astype(jnp.float32)))[:, :1]

    def weighted(share, which, step, cols):
        value = share * grads[which, step, :, cols].astype(jnp.float32)
        return value.astype(jnp.bfloat16)

    for which in range(CORES):
        for step in range(ring):
            slab(which, step).wait()
    pl.semaphore_wait(barrier, 1 + ring - 1 + shards - 1)

    def pair_copy(p):
        return remote(
            pair_out.at[:, :, piece_of(p)],
            pair_in.at[:, :, piece_of(p)],
            pair_send,
            pair_recv.at[p],
            "ep",
            partner,
        )

    def give():
        shares = [share_of(group_of(step, 1 - core)) for step in range(ring)]

        def body(p, carry):
            def weigh(i, inner):
                cols = cols_of(p, i)
                for step in range(ring):
                    pair_out[step, :, cols] = weighted(shares[step], 1 - core, step, cols)
                return inner

            lax.fori_loop(0, piece // narrow, weigh, 0)
            pair_copy(p).start()
            return carry

        lax.fori_loop(0, pieces, body, 0)

    def ring_copy(step, p):
        return remote(
            ring_out.at[step - 1, :, piece_of(p)],
            ring_in.at[step - 1, :, piece_of(p)],
            ring_send.at[step - 1],
            ring_recv.at[step - 1, p],
            "ep",
            group_of(step, core),
        )

    @pl.when(core == 1)
    def _():
        give()
        pl.semaphore_wait(gate, 1)

    shares = [share_of(group_of(step, core)) for step in range(ring)]
    order = sorted(range(1, ring), key=lambda step: abs(2 * step - ring))

    def send_piece(p, carry):
        pair_copy(p).wait_recv()
        for step in order:

            def add(i, inner, step=step):
                cols = cols_of(p, i)
                total = weighted(shares[step], core, step, cols).astype(jnp.float32)
                total = total + pair_in[step, :, cols].astype(jnp.float32)
                ring_out[step - 1, :, cols] = total.astype(jnp.bfloat16)
                return inner

            lax.fori_loop(0, piece // narrow, add, 0)
            ring_copy(step, p).start()
        return carry

    lax.fori_loop(0, pieces, send_piece, 0)

    @pl.when(core == 0)
    def _():
        give()

    for copy in params:
        copy.wait()

    def moments(p, carry):
        for step in range(1, ring):
            ring_copy(step, p).wait_recv()

        @pl.when(jnp.logical_and(core == 0, p == GATE_PIECE))
        def _():
            pl.semaphore_signal(
                gate,
                inc=1,
                device_id={"ep": partner},
                device_id_type=pl.DeviceIdType.MESH,
            )

        def one(i, inner):
            grad_acc, mom_acc = inner
            cols = cols_of(p, i)
            total = weighted(shares[0], core, 0, cols).astype(jnp.float32)
            total = total + pair_in[0, :, cols].astype(jnp.float32)
            for step in range(1, ring):
                total = total + ring_in[step - 1, :, cols].astype(jnp.float32)
            mom_next = MOMENTUM_DECAY * mom[:, cols] + (1.0 - MOMENTUM_DECAY) * total
            gradient[:, cols] = total
            mom[:, cols] = mom_next
            second[:, cols] = (
                SECOND_DECAY * second[:, cols] + (1.0 - SECOND_DECAY) * total * total
            )
            return grad_acc + total * total, mom_acc + mom_next * mom_next

        return lax.fori_loop(0, piece // narrow, one, carry)

    zero = jnp.zeros((rows, narrow), jnp.float32)
    grad_acc, mom_acc = lax.fori_loop(0, pieces, moments, (zero, zero))

    def to_lanes(acc):
        acc = jnp.sum(acc, axis=0, keepdims=True)
        return sum(acc[:, j : j + LANES] for j in range(0, narrow, LANES))

    sums[me, 0:1, :] = to_lanes(grad_acc)
    sums[me, 1:2, :] = to_lanes(mom_acc)
    sum_sends = []
    for step in range(1, shards):
        copy = remote(
            sums.at[me],
            sums.at[me],
            sum_send.at[step - 1],
            sum_recv.at[me],
            "fs",
            (me + step) % shards,
        )
        copy.start()
        sum_sends.append(copy)
    for step in range(1, shards):
        source = (me + step) % shards
        remote(
            sums.at[source],
            sums.at[source],
            sum_send.at[step - 1],
            sum_recv.at[source],
            "fs",
            source,
        ).wait_recv()

    entries = rows * columns * shards
    totals = sums[0]
    for s in range(1, shards):
        totals = totals + sums[s]
    mean = jnp.broadcast_to(jnp.sum(totals, axis=1, keepdims=True) / entries, (2, LANES)) + NORM_EPS
    inverse = lax.rsqrt(mean)
    inv_grad = inverse[0:1, :1]
    inv_mom = inverse[1:2, :1]
    log_mom = jnp.max(0.5 * jnp.log(mean[1:2, :]))
    for h in range(units):
        bias[h] = in_bias[h] + in_weight[5, h] * log_mom

    chunks = pass_recv.shape[1]
    width = columns // chunks
    tile = tile_width(width, 256)

    def learned_step(cols):
        grad = gradient[:, cols]
        mom_next = mom[:, cols]
        old = weight[:, cols].astype(jnp.float32)
        inv_root = lax.rsqrt(second[:, cols] + ROOT_EPS)
        features = (
            grad * inv_grad,
            mom_next * inv_mom,
            mom_next * inv_root,
            grad * inv_root,
            old,
        )
        direction = jnp.full(grad.shape, out_bias[0])
        magnitude = jnp.full(grad.shape, out_bias[1])
        for h in range(units):
            hidden = features[0] * in_weight[0, h] + bias[h]
            for f in range(1, len(features)):
                hidden = hidden + features[f] * in_weight[f, h]
            hidden = jnp.maximum(hidden, 0.0)
            direction = direction + hidden * out_weight[0, h]
            magnitude = magnitude + hidden * out_weight[1, h]
        update = STEP_SCALE * direction * jnp.exp(EXP_SCALE * magnitude)
        return (old - update).astype(jnp.bfloat16)

    def rows_of(source):
        return pl.ds(pl.multiple_of(source * rows, rows), rows)

    def block(source, k):
        return gathered.at[rows_of(source), pl.ds(pl.multiple_of(k * width, width), width)]

    def route(k):
        swap = k % 2
        turn = 1 - 2 * (k // 2 % 2)

        def at(first, after):
            up = (z + 2 * SIDE + first * swap + after * (1 - swap)) % SIDE
            along = (x + 2 * SIDE + first * (1 - swap) + after * swap) % SIDE
            return up * SIDE + along

        return at, turn

    def send(source, k, role, recv, peer):
        remote(block(source, k), block(source, k), row_send.at[role], recv, "fs", peer).start()

    def spread(source, k, role, at, turn):
        send(source, k, role, pass_recv.at[source, k], at(0, turn))
        send(source, k, role, last_recv.at[source], at(0, -turn))

    def arrive(source, k):
        remote(
            block(source, k), block(source, k), row_send.at[0], pass_recv.at[source, k], "fs", source
        ).wait_recv()

    def own(k):
        at, turn = route(k)
        for way in (1, -1):
            send(me, k, 0, pass_recv.at[me, k], at(way, 0))
        spread(me, k, 0, at, turn)

    def relay_one(k):
        at, turn = route(k)
        source = at(-turn, 0)
        arrive(source, k)
        send(source, k, 1, pass_recv.at[source, k], at(turn, 0))
        spread(source, k, 1, at, turn)
        source = at(turn, 0)
        arrive(source, k)
        spread(source, k, 1, at, turn)
        source = at(0, -turn)
        arrive(source, k)
        send(source, k, 1, last_recv.at[source], at(0, turn))

    def relay_two(k):
        at, turn = route(k)
        source = at(2, 0)
        arrive(source, k)
        spread(source, k, 2, at, turn)
        for way in (1, -1):
            source = at(way, -turn)
            arrive(source, k)
            send(source, k, 2, last_recv.at[source], at(0, turn))

    def relay_three(k):
        at, turn = route(k)
        source = at(2, -turn)
        arrive(source, k)
        send(source, k, 3, last_recv.at[source], at(0, turn))

    def turn_of(t, carry):
        for lag, relay in ((LAG_ONE, relay_one), (LAG_TWO, relay_two), (LAG_THREE, relay_three)):
            k = t - lag

            @pl.when(jnp.logical_and(k >= 0, k < chunks))
            def _(k=k, relay=relay):
                relay(k)

        @pl.when(t < chunks)
        def _():
            def one(i, inner):
                cols = pl.ds(pl.multiple_of(t * width + i * tile, tile), tile)
                gathered[rows_of(me), cols] = learned_step(cols)
                return inner

            lax.fori_loop(0, width // tile, one, 0)
            own(t)

        return carry

    lax.fori_loop(0, chunks + LAG_THREE, turn_of, 0)

    remote(pair_out, pair_in, pair_send, pair_recv.at[0], "ep", partner).wait_send()
    for step in range(1, ring):
        remote(
            ring_out.at[step - 1],
            ring_in.at[step - 1],
            ring_send.at[step - 1],
            ring_recv.at[step - 1, 0],
            "ep",
            group_of(step, core),
        ).wait_send()
    for copy in sum_sends:
        copy.wait_send()
    share = {0: 0, 1: chunks // 4, 2: chunks // 2, 3: chunks // 4}
    for up in range(SIDE):
        for along in range(SIDE):
            number = share[up] + share[along]
            if number == 0:
                continue
            source = (z + up) % SIDE * SIDE + (x + along) % SIDE
            part = gathered.at[rows_of(source), pl.ds(0, number * width)]
            remote(part, part, row_send.at[0], last_recv.at[source], "fs", source).wait_recv()
    for role, number in enumerate((4, 6, 4, 1)):
        part = gathered.at[pl.ds(0, number * rows), :]
        remote(
            part, part, row_send.at[role], last_recv.at[me], "fs", (me + 1) % shards
        ).wait_send()


def per_device(groups, grads, counts, weight, mom, second, in_weight, in_bias, out_weight, out_bias):
    rows, columns = mom.shape[1], mom.shape[2]
    ring = groups // CORES
    shards = SIDE * SIDE
    pieces = PIECES
    chunks = CHUNKS
    hbm = pl.BlockSpec(memory_space=pltpu.HBM)
    vmem = pl.BlockSpec(memory_space=pltpu.VMEM)
    return pl.pallas_call(
        functools.partial(kernel, ring),
        out_shape=(
            pltpu.VMEM((1, rows * shards, columns), jnp.bfloat16),
            pltpu.VMEM(mom.shape, jnp.float32),
            pltpu.VMEM(second.shape, jnp.float32),
        ),
        in_specs=[hbm] * 9,
        out_specs=(vmem, vmem, vmem),
        scratch_shapes=[
            pltpu.SMEM(counts.shape, jnp.int32),
            pltpu.SMEM(in_weight.shape, jnp.float32),
            pltpu.SMEM(in_bias.shape, jnp.float32),
            pltpu.SMEM(out_weight.shape[::-1], jnp.float32),
            pltpu.SMEM(out_bias.shape, jnp.float32),
            pltpu.VMEM((CORES, ring, rows, columns), jnp.bfloat16),
            pltpu.VMEM((rows, columns), jnp.bfloat16),
            pltpu.VMEM((ring, rows, columns), jnp.bfloat16),
            pltpu.VMEM((ring, rows, columns), jnp.bfloat16),
            pltpu.VMEM((ring - 1, rows, columns), jnp.bfloat16),
            pltpu.VMEM((ring - 1, rows, columns), jnp.bfloat16),
            pltpu.VMEM((rows, columns), jnp.float32),
            pltpu.VMEM((shards, 2, LANES), jnp.float32),
            pltpu.SMEM((in_bias.shape[0],), jnp.float32),
            pltpu.SemaphoreType.DMA((5,)),
            pltpu.SemaphoreType.DMA((CORES, ring)),
            pltpu.SemaphoreType.DMA((3,)),
            pltpu.SemaphoreType.DMA,
            pltpu.SemaphoreType.DMA((pieces,)),
            pltpu.SemaphoreType.DMA((ring - 1,)),
            pltpu.SemaphoreType.DMA((ring - 1, pieces)),
            pltpu.SemaphoreType.REGULAR,
            pltpu.SemaphoreType.DMA((shards - 1,)),
            pltpu.SemaphoreType.DMA((shards,)),
            pltpu.SemaphoreType.DMA((4,)),
            pltpu.SemaphoreType.DMA((shards, chunks)),
            pltpu.SemaphoreType.DMA((shards,)),
        ],
        compiler_params=pltpu.CompilerParams(
            collective_id=0, has_side_effects=True, vmem_limit_bytes=VMEM_BYTES
        ),
        name="learned_update",
    )(counts, in_weight, in_bias, out_weight.T, out_bias, grads, weight, mom, second)


def solution(mesh):
    in_specs = (
        P("ep", None, "fs", None),
        P(),
        P("ep", "fs", None),
        P("ep", "fs", None),
        P("ep", "fs", None),
        P(),
        P(),
        P(),
        P(),
    )
    out_specs = (P("ep", None, None), P("ep", "fs", None), P("ep", "fs", None))
    body = functools.partial(per_device, mesh.shape["ep"])
    return jax.shard_map(
        body, mesh=mesh, in_specs=in_specs, out_specs=out_specs, check_vma=False
    )
```

time: 175 us -> 85.5 us (0.49)
  the two profiles are of different devices: /device:TPU:0 before, /device:TPU:1 now
where the time goes in v1:
time: 85.5 us; the launch traced here: 85.4 us
  Pallas kernels  79.8 us (93%)
  local copies, waits for them, and re-layouts  4.89 us (6%)
    pallas_call x1, Pallas kernels, per_device(): pl.pallas_call(functools.partial(kernel, ring), out_shape=(pltpu.VMEM((1,...  79.8 us
    unnamed x3, local copies, waits for them, and re-layouts  4.89 us

profile of v1, /device:TPU:1, one launch (start us, length us, event | category | flops | bytes accessed | tf_op | source)
XLA Modules:
  0.0 85.4 jit_solution(5917846336791748260)
XLA Ops:
  0.6 79.8 %learned_update.1 = (bf16[1,256,14336]{2,1,0:T(8,128)(2,1)S(1)}, f32[1,16,14336]{2,1,0:T(8,128)S(1)}, f32[1,16,14336]{2,1,0:T(8,128)S(1)}) custom-call(s32[8,8]{1,0:T(8,128)} %counts_hbm.1, f32[6,32]{1,0:T(8,128)} %in_weight_hbm.1, f32[32]{0:T(128)} %in_bias_hbm.1, f32[2,32]{1,0:T(2,128)} %bitcast.1, f32[2]{0:T(128)} %out_bias_hbm.1, ...), custom_call_target="tpu_custom_call" | custom-call | tf_op jit(solution)/shard_map/learned_update/pallas_call | solution.py:474
  80.5 3.1 %copy.15 = bf16[1,256,14336]{2,1,0:T(8,128)(2,1)} copy(bf16[1,256,14336]{2,1,0:T(8,128)(2,1)S(1)} %get-tuple-element.3) | data formatting | bytes 14680064
  83.5 0.9 %copy.16 = f32[1,16,14336]{2,1,0:T(8,128)} copy(f32[1,16,14336]{2,1,0:T(8,128)S(1)} %get-tuple-element.4) | data formatting | bytes 1835008
  84.5 0.9 %copy.17 = f32[1,16,14336]{2,1,0:T(8,128)} copy(f32[1,16,14336]{2,1,0:T(8,128)S(1)} %get-tuple-element.5) | data formatting | bytes 1835008

commit v2 on v1

--- a/solution.py
+++ b/solution.py
@@ -18,10 +18,15 @@
 SIDE = 4
 CHUNKS = 16
 PIECES = 7
-LAG_ONE = 3
-LAG_TWO = 6
-LAG_THREE = 9
+LAG_ONE = 5
+LAG_TWO = 10
+LAG_THREE = 15
 GATE_PIECE = 5
+FIRST = 1
+CODES = 32767.0
+TINY = 1e-30
+TILE = 896
+STORES = 4
 VMEM_BYTES = 67043328 - 9175040
 
 
@@ -69,9 +74,11 @@
     pair_in,
     ring_out,
     ring_in,
+    scale_out,
+    scale_in,
     gradient,
     sums,
-    bias,
+    layer,
     small_sem,
     slab_sem,
     param_sem,
@@ -79,6 +86,8 @@
     pair_recv,
     ring_send,
     ring_recv,
+    scale_send,
+    scale_recv,
     gate,
     sum_send,
     sum_recv,
@@ -126,7 +135,7 @@
             slab_sem.at[which, step],
         )
 
-    for which in range(CORES):
+    for which in (FIRST, 1 - FIRST):
         for step in range(ring):
             slab(which, step).start()
     params = [
@@ -215,7 +224,7 @@
             group_of(step, core),
         )
 
-    @pl.when(core == 1)
+    @pl.when(core != FIRST)
     def _():
         give()
         pl.semaphore_wait(gate, 1)
@@ -223,35 +232,77 @@
     shares = [share_of(group_of(step, core)) for step in range(ring)]
     order = sorted(range(1, ring), key=lambda step: abs(2 * step - ring))
 
+    def scale_copy(step, p):
+        return remote(
+            scale_out.at[step - 1, p],
+            scale_in.at[step - 1, p],
+            scale_send.at[step - 1],
+            scale_recv.at[step - 1, p],
+            "ep",
+            group_of(step, core),
+        )
+
+    def spread_lanes(row, width):
+        return jnp.concatenate([row] * (width // LANES), axis=1)
+
     def send_piece(p, carry):
         pair_copy(p).wait_recv()
+        cols = piece_of(p)
         for step in order:
-
-            def add(i, inner, step=step):
-                cols = cols_of(p, i)
-                total = weighted(shares[step], core, step, cols).astype(jnp.float32)
-                total = total + pair_in[step, :, cols].astype(jnp.float32)
-                ring_out[step - 1, :, cols] = total.astype(jnp.bfloat16)
-                return inner
-
-            lax.fori_loop(0, piece // narrow, add, 0)
+            total = weighted(shares[step], core, step, cols).astype(jnp.float32)
+            total = total + pair_in[step, :, cols].astype(jnp.float32)
+            most = jnp.max(jnp.abs(total), axis=0, keepdims=True)
+            parts = [most[:, j : j + LANES] for j in range(0, piece, LANES)]
+            most = jnp.maximum(functools.reduce(jnp.maximum, parts), TINY)
+            scale_out[step - 1, p] = most * (1.0 / CODES)
+            codes = lax.round(
+                total * spread_lanes(CODES / most, piece), lax.RoundingMethod.TO_NEAREST_EVEN
+            )
+            ring_out[step - 1, :, cols] = codes.astype(jnp.int32).astype(jnp.int16)
             ring_copy(step, p).start()
+            scale_copy(step, p).start()
         return carry
 
     lax.fori_loop(0, pieces, send_piece, 0)
 
-    @pl.when(core == 0)
+    @pl.when(core == FIRST)
     def _():
         give()
 
+    shape = (rows, layer.shape[1])
+    lane = lax.broadcasted_iota(jnp.int32, shape, 1)
+    slot = lane // rows
+    diagonal = lane % rows == lax.broadcasted_iota(jnp.int32, shape, 0)
+
+    def halves(value):
+        high = value.astype(jnp.bfloat16).astype(jnp.float32)
+        return high, value - high
+
+    def place(h, carry):
+        block = jnp.zeros(shape, jnp.float32)
+        for f in range(5):
+            high, low = halves(jnp.full(shape, in_weight[f, h]))
+            whole = slot == f
+            if f < 4:
+                whole = jnp.logical_or(whole, slot == 5 + f)
+            block = jnp.where(whole, high, jnp.where(slot == 9 + f, low, block))
+        block = jnp.where(diagonal, block, 0.0)
+        layer[pl.ds(pl.multiple_of(h * rows, rows), rows), :] = block.astype(jnp.bfloat16)
+        return carry
+
+    lax.fori_loop(0, units, place, 0)
     for copy in params:
         copy.wait()
 
     def moments(p, carry):
         for step in range(1, ring):
             ring_copy(step, p).wait_recv()
-
-        @pl.when(jnp.logical_and(core == 0, p == GATE_PIECE))
+            scale_copy(step, p).wait_recv()
+        scales = [
+            spread_lanes(scale_in[step - 1, p], narrow) for step in range(1, ring)
+        ]
+
+        @pl.when(jnp.logical_and(core == FIRST, p == GATE_PIECE))
         def _():
             pl.semaphore_signal(
                 gate,
@@ -266,7 +317,8 @@
             total = weighted(shares[0], core, 0, cols).astype(jnp.float32)
             total = total + pair_in[0, :, cols].astype(jnp.float32)
             for step in range(1, ring):
-                total = total + ring_in[step - 1, :, cols].astype(jnp.float32)
+                codes = ring_in[step - 1, :, cols].astype(jnp.int32).astype(jnp.float32)
+                total = total + codes * scales[step - 1]
             mom_next = MOMENTUM_DECAY * mom[:, cols] + (1.0 - MOMENTUM_DECAY) * total
             gradient[:, cols] = total
             mom[:, cols] = mom_next
@@ -286,28 +338,13 @@
 
     sums[me, 0:1, :] = to_lanes(grad_acc)
     sums[me, 1:2, :] = to_lanes(mom_acc)
-    sum_sends = []
     for step in range(1, shards):
-        copy = remote(
-            sums.at[me],
-            sums.at[me],
-            sum_send.at[step - 1],
-            sum_recv.at[me],
-            "fs",
-            (me + step) % shards,
-        )
-        copy.start()
-        sum_sends.append(copy)
-    for step in range(1, shards):
-        source = (me + step) % shards
         remote(
-            sums.at[source],
-            sums.at[source],
-            sum_send.at[step - 1],
-            sum_recv.at[source],
-            "fs",
-            source,
-        ).wait_recv()
+            sums.at[me], sums.at[me], sum_send, sum_recv, "fs", (me + step) % shards
+        ).start()
+    others = sums.at[pl.ds(0, shards - 1)]
+    all_sums = remote(others, others, sum_send, sum_recv, "fs", (me + 1) % shards)
+    all_sums.wait_recv()
 
     entries = rows * columns * shards
     totals = sums[0]
@@ -318,36 +355,55 @@
     inv_grad = inverse[0:1, :1]
     inv_mom = inverse[1:2, :1]
     log_mom = jnp.max(0.5 * jnp.log(mean[1:2, :]))
-    for h in range(units):
-        bias[h] = in_bias[h] + in_weight[5, h] * log_mom
+    tail = pl.ds(shape[1] - LANES, LANES)
+    biased = slot[:, -LANES:] >= 14
+    first = slot[:, -LANES:] == 14
+    ends = diagonal[:, -LANES:]
+
+    def settle(h, carry):
+        high, low = halves(jnp.full(ends.shape, in_bias[h] + in_weight[5, h] * log_mom))
+        span = pl.ds(pl.multiple_of(h * rows, rows), rows)
+        block = jnp.where(ends, jnp.where(first, high, low), 0.0)
+        kept = layer[span, tail].astype(jnp.float32)
+        layer[span, tail] = jnp.where(biased, block, kept).astype(jnp.bfloat16)
+        return carry
+
+    lax.fori_loop(0, units, settle, 0)
 
     chunks = pass_recv.shape[1]
     width = columns // chunks
-    tile = tile_width(width, 256)
+    tile = tile_width(width, TILE)
 
     def learned_step(cols):
         grad = gradient[:, cols]
         mom_next = mom[:, cols]
-        old = weight[:, cols].astype(jnp.float32)
+        narrow_old = weight[:, cols]
         inv_root = lax.rsqrt(second[:, cols] + ROOT_EPS)
-        features = (
+        highs, lows = [], []
+        for value in (
             grad * inv_grad,
             mom_next * inv_mom,
             mom_next * inv_root,
             grad * inv_root,
-            old,
-        )
-        direction = jnp.full(grad.shape, out_bias[0])
-        magnitude = jnp.full(grad.shape, out_bias[1])
+        ):
+            high = value.astype(jnp.bfloat16)
+            highs.append(high)
+            lows.append((value - high.astype(jnp.float32)).astype(jnp.bfloat16))
+        highs.append(narrow_old)
+        ones = jnp.ones(grad.shape, jnp.bfloat16)
+        features = jnp.concatenate(highs + lows + highs + [ones, ones], axis=0)
+        hidden = jnp.dot(layer[...], features, preferred_element_type=jnp.float32)
+        directions = [jnp.full(grad.shape, out_bias[0]), jnp.zeros(grad.shape, jnp.float32)]
+        magnitudes = [jnp.full(grad.shape, out_bias[1]), jnp.zeros(grad.shape, jnp.float32)]
         for h in range(units):
-            hidden = features[0] * in_weight[0, h] + bias[h]
-            for f in range(1, len(features)):
-                hidden = hidden + features[f] * in_weight[f, h]
-            hidden = jnp.maximum(hidden, 0.0)
-            direction = direction + hidden * out_weight[0, h]
-            magnitude = magnitude + hidden * out_weight[1, h]
+            active = jnp.maximum(hidden[h * rows : (h + 1) * rows, :], 0.0)
+            side = 2 * h // units
+            directions[side] = directions[side] + active * out_weight[0, h]
+            magnitudes[side] = magnitudes[side] + active * out_weight[1, h]
+        direction = directions[0] + directions[1]
+        magnitude = magnitudes[0] + magnitudes[1]
         update = STEP_SCALE * direction * jnp.exp(EXP_SCALE * magnitude)
-        return (old - update).astype(jnp.bfloat16)
+        return (narrow_old.astype(jnp.float32) - update).astype(jnp.bfloat16)
 
     def rows_of(source):
         return pl.ds(pl.multiple_of(source * rows, rows), rows)
@@ -369,49 +425,49 @@
     def send(source, k, role, recv, peer):
         remote(block(source, k), block(source, k), row_send.at[role], recv, "fs", peer).start()
 
-    def spread(source, k, role, at, turn):
-        send(source, k, role, pass_recv.at[source, k], at(0, turn))
-        send(source, k, role, last_recv.at[source], at(0, -turn))
-
-    def arrive(source, k):
+    def spread(source, k, role, part, at, way):
+        send(source, k, role, pass_recv.at[part, k], at(0, way))
+        send(source, k, role, last_recv.at[source], at(0, -way))
+
+    def arrive(source, k, part):
         remote(
-            block(source, k), block(source, k), row_send.at[0], pass_recv.at[source, k], "fs", source
+            block(source, k), block(source, k), row_send.at[0], pass_recv.at[part, k], "fs", source
         ).wait_recv()
 
     def own(k):
         at, turn = route(k)
-        for way in (1, -1):
-            send(me, k, 0, pass_recv.at[me, k], at(way, 0))
-        spread(me, k, 0, at, turn)
+        send(me, k, 0, pass_recv.at[0, k], at(turn, 0))
+        send(me, k, 0, pass_recv.at[1, k], at(-turn, 0))
+        spread(me, k, 0, 3, at, turn)
+
+    def pass_on(k, role, first, part):
+        at, turn = route(k)
+        way = turn if first % 2 == 0 else -turn
+        source = at(first * turn, -way)
+        arrive(source, k, part)
+        send(source, k, role, last_recv.at[source], at(0, way))
 
     def relay_one(k):
         at, turn = route(k)
         source = at(-turn, 0)
-        arrive(source, k)
-        send(source, k, 1, pass_recv.at[source, k], at(turn, 0))
-        spread(source, k, 1, at, turn)
+        arrive(source, k, 0)
+        send(source, k, 1, pass_recv.at[2, k], at(turn, 0))
+        spread(source, k, 1, 4, at, -turn)
         source = at(turn, 0)
-        arrive(source, k)
-        spread(source, k, 1, at, turn)
-        source = at(0, -turn)
-        arrive(source, k)
-        send(source, k, 1, last_recv.at[source], at(0, turn))
+        arrive(source, k, 1)
+        spread(source, k, 1, 5, at, -turn)
+        pass_on(k, 1, 0, 3)
 
     def relay_two(k):
         at, turn = route(k)
         source = at(2, 0)
-        arrive(source, k)
-        spread(source, k, 2, at, turn)
-        for way in (1, -1):
-            source = at(way, -turn)
-            arrive(source, k)
-            send(source, k, 2, last_recv.at[source], at(0, turn))
+        arrive(source, k, 2)
+        spread(source, k, 2, 6, at, turn)
+        pass_on(k, 2, -1, 4)
+        pass_on(k, 2, 1, 5)
 
     def relay_three(k):
-        at, turn = route(k)
-        source = at(2, -turn)
-        arrive(source, k)
-        send(source, k, 3, last_recv.at[source], at(0, turn))
+        pass_on(k, 3, 2, 6)
 
     def turn_of(t, carry):
         for lag, relay in ((LAG_ONE, relay_one), (LAG_TWO, relay_two), (LAG_THREE, relay_three)):
@@ -445,8 +501,15 @@
             "ep",
             group_of(step, core),
         ).wait_send()
-    for copy in sum_sends:
-        copy.wait_send()
+        remote(
+            scale_out.at[step - 1],
+            scale_in.at[step - 1],
+            scale_send.at[step - 1],
+            scale_recv.at[step - 1, 0],
+            "ep",
+            group_of(step, core),
+        ).wait_send()
+    all_sums.wait_send()
     share = {0: 0, 1: chunks // 4, 2: chunks // 2, 3: chunks // 4}
     for up in range(SIDE):
         for along in range(SIDE):
@@ -463,6 +526,24 @@
         ).wait_send()
 
 
+def store(gathered, mom, second, gathered_hbm, mom_hbm, second_hbm, sems):
+    height = gathered.shape[1] // STORES
+    copies = [
+        pltpu.make_async_copy(
+            gathered.at[:, pl.ds(i * height, height), :],
+            gathered_hbm.at[:, pl.ds(i * height, height), :],
+            sems.at[i],
+        )
+        for i in range(STORES)
+    ]
+    copies.append(pltpu.make_async_copy(mom, mom_hbm, sems.at[STORES]))
+    copies.append(pltpu.make_async_copy(second, second_hbm, sems.at[STORES + 1]))
+    for copy in copies:
+        copy.start()
+    for copy in copies:
+        copy.wait()
+
+
 def per_device(groups, grads, counts, weight, mom, second, in_weight, in_bias, out_weight, out_bias):
     rows, columns = mom.shape[1], mom.shape[2]
     ring = groups // CORES
@@ -471,7 +552,7 @@
     chunks = CHUNKS
     hbm = pl.BlockSpec(memory_space=pltpu.HBM)
     vmem = pl.BlockSpec(memory_space=pltpu.VMEM)
-    return pl.pallas_call(
+    results = pl.pallas_call(
         functools.partial(kernel, ring),
         out_shape=(
             pltpu.VMEM((1, rows * shards, columns), jnp.bfloat16),
@@ -490,11 +571,13 @@
             pltpu.VMEM((rows, columns), jnp.bfloat16),
             pltpu.VMEM((ring, rows, columns), jnp.bfloat16),
             pltpu.VMEM((ring, rows, columns), jnp.bfloat16),
-            pltpu.VMEM((ring - 1, rows, columns), jnp.bfloat16),
-            pltpu.VMEM((ring - 1, rows, columns), jnp.bfloat16),
+            pltpu.VMEM((ring - 1, rows, columns), jnp.int16),
+            pltpu.VMEM((ring - 1, rows, columns), jnp.int16),
+            pltpu.VMEM((ring - 1, pieces, 1, LANES), jnp.float32),
+            pltpu.VMEM((ring - 1, pieces, 1, LANES), jnp.float32),
             pltpu.VMEM((rows, columns), jnp.float32),
             pltpu.VMEM((shards, 2, LANES), jnp.float32),
-            pltpu.SMEM((in_bias.shape[0],), jnp.float32),
+            pltpu.VMEM((in_bias.shape[0] * rows, 16 * rows), jnp.bfloat16),
             pltpu.SemaphoreType.DMA((5,)),
             pltpu.SemaphoreType.DMA((CORES, ring)),
             pltpu.SemaphoreType.DMA((3,)),
@@ -502,11 +585,13 @@
             pltpu.SemaphoreType.DMA((pieces,)),
             pltpu.SemaphoreType.DMA((ring - 1,)),
             pltpu.SemaphoreType.DMA((ring - 1, pieces)),
+            pltpu.SemaphoreType.DMA((ring - 1,)),
+            pltpu.SemaphoreType.DMA((ring - 1, pieces)),
             pltpu.SemaphoreType.REGULAR,
-            pltpu.SemaphoreType.DMA((shards - 1,)),
-            pltpu.SemaphoreType.DMA((shards,)),
+            pltpu.SemaphoreType.DMA,
+            pltpu.SemaphoreType.DMA,
             pltpu.SemaphoreType.DMA((4,)),
-            pltpu.SemaphoreType.DMA((shards, chunks)),
+            pltpu.SemaphoreType.DMA((7, chunks)),
             pltpu.SemaphoreType.DMA((shards,)),
         ],
         compiler_params=pltpu.CompilerParams(
@@ -514,6 +599,15 @@
         ),
         name="learned_update",
     )(counts, in_weight, in_bias, out_weight.T, out_bias, grads, weight, mom, second)
+    return pl.pallas_call(
+        store,
+        out_shape=[jax.ShapeDtypeStruct(r.shape, r.dtype) for r in results],
+        in_specs=[vmem] * 3,
+        out_specs=[hbm] * 3,
+        scratch_shapes=[pltpu.SemaphoreType.DMA((STORES + 2,))],
+        compiler_params=pltpu.CompilerParams(vmem_limit_bytes=1024 * 1024),
+        name="store_results",
+    )(*results)
 
 
 def solution(mesh):

time: 85.5 us -> 76.6 us (0.90)
  the two profiles are of different devices: /device:TPU:1 before, /device:TPU:0 now
where the time goes in v2:
time: 76.6 us; the launch traced here: 76.5 us
  Pallas kernels  75.9 us (99%)
    pallas_call x1, Pallas kernels, per_device(): pl.pallas_call(functools.partial(kernel, ring), out_shape=(pltpu.VMEM((1,...  72.2 us
    pallas_call x1, Pallas kernels, per_device(): pl.pallas_call(store, out_shape=[jax.ShapeDtypeStruct(r.shape, r.dtype) f...  3.62 us

profile of v2, /device:TPU:0, one launch (start us, length us, event | category | flops | bytes accessed | tf_op | source)
XLA Modules:
  0.0 76.5 jit_solution(16434382376449004846)
XLA Ops:
  0.6 72.2 %learned_update.1 = (bf16[1,256,14336]{2,1,0:T(8,128)(2,1)S(1)}, f32[1,16,14336]{2,1,0:T(8,128)S(1)}, f32[1,16,14336]{2,1,0:T(8,128)S(1)}) custom-call(s32[8,8]{1,0:T(8,128)} %counts_hbm.1, f32[6,32]{1,0:T(8,128)} %in_weight_hbm.1, f32[32]{0:T(128)} %in_bias_hbm.1, f32[2,32]{1,0:T(2,128)} %bitcast.1, f32[2]{0:T(128)} %out_bias_hbm.1, ...), custom_call_target="tpu_custom_call" | custom-call | tf_op jit(solution)/shard_map/learned_update/pallas_call | solution.py:555
  72.9 3.6 %store_results.1 = (bf16[1,256,14336]{2,1,0:T(8,128)(2,1)}, f32[1,16,14336]{2,1,0:T(8,128)}, f32[1,16,14336]{2,1,0:T(8,128)}) custom-call(bf16[1,256,14336]{2,1,0:T(8,128)(2,1)S(1)} %get-tuple-element.6.gathered, f32[1,16,14336]{2,1,0:T(8,128)S(1)} %get-tuple-element.7.mom, f32[1,16,14336]{2,1,0:T(8,128)S(1)} %get-tuple-element.8.second), custom_call_target="tpu_custom_call" | custom-call | tf_op jit(solution)/shard_map/store_results/pallas_call | solution.py:602

commit v3 on v2

--- a/solution.py
+++ b/solution.py
@@ -17,12 +17,13 @@
 CORES = 2
 SIDE = 4
 CHUNKS = 16
-PIECES = 7
-LAG_ONE = 5
-LAG_TWO = 10
-LAG_THREE = 15
-GATE_PIECE = 5
+PIECES = 8
+LAG_ONE = 6
+LAG_TWO = 11
+LAG_THREE = 16
+GATE_PIECE = 6
 FIRST = 1
+ORDER = (2, 1, 3, 0)
 CODES = 32767.0
 TINY = 1e-30
 TILE = 896
@@ -79,6 +80,7 @@
     gradient,
     sums,
     layer,
+    tally,
     small_sem,
     slab_sem,
     param_sem,
@@ -87,7 +89,6 @@
     ring_send,
     ring_recv,
     scale_send,
-    scale_recv,
     gate,
     sum_send,
     sum_recv,
@@ -132,21 +133,17 @@
         return pltpu.make_async_copy(
             grads_hbm.at[0, group_of(step, which)],
             grads.at[which, step],
-            slab_sem.at[which, step],
-        )
+            slab_sem.at[which],
+        )
+
+    def slabs_in(which):
+        pltpu.make_async_copy(
+            grads_hbm.at[0, pl.ds(0, ring)], grads.at[which], slab_sem.at[which]
+        ).wait()
 
     for which in (FIRST, 1 - FIRST):
-        for step in range(ring):
+        for step in ORDER:
             slab(which, step).start()
-    params = [
-        pltpu.make_async_copy(src.at[0], dst, param_sem.at[i])
-        for i, (src, dst) in enumerate(
-            ((mom_hbm, mom), (second_hbm, second), (weight_hbm, weight))
-        )
-    ]
-    for copy in params:
-        copy.start()
-
     barrier = pltpu.get_barrier_semaphore()
     for peer in [partner] + [group_of(step, core) for step in range(1, ring)]:
         pl.semaphore_signal(
@@ -159,8 +156,7 @@
             device_id={"fs": (me + step) % shards},
             device_id_type=pl.DeviceIdType.MESH,
         )
-    for copy in small:
-        copy.wait()
+    small[0].wait()
 
     pieces = ring_recv.shape[1]
     piece = columns // pieces
@@ -183,46 +179,80 @@
         value = share * grads[which, step, :, cols].astype(jnp.float32)
         return value.astype(jnp.bfloat16)
 
-    for which in range(CORES):
-        for step in range(ring):
-            slab(which, step).wait()
+    slabs_in(FIRST)
     pl.semaphore_wait(barrier, 1 + ring - 1 + shards - 1)
 
-    def pair_copy(p):
+    def pair_copy(part, p):
+        slots = (pl.ds(0, 1), pl.ds(1, ring - 1))[part]
         return remote(
-            pair_out.at[:, :, piece_of(p)],
-            pair_in.at[:, :, piece_of(p)],
-            pair_send,
-            pair_recv.at[p],
+            pair_out.at[slots, :, piece_of(p)],
+            pair_in.at[slots, :, piece_of(p)],
+            pair_send.at[part],
+            pair_recv.at[part, p],
             "ep",
             partner,
         )
 
     def give():
         shares = [share_of(group_of(step, 1 - core)) for step in range(ring)]
-
-        def body(p, carry):
-            def weigh(i, inner):
-                cols = cols_of(p, i)
-                for step in range(ring):
-                    pair_out[step, :, cols] = weighted(shares[step], 1 - core, step, cols)
-                return inner
-
-            lax.fori_loop(0, piece // narrow, weigh, 0)
-            pair_copy(p).start()
-            return carry
-
-        lax.fori_loop(0, pieces, body, 0)
-
-    def ring_copy(step, p):
-        return remote(
-            ring_out.at[step - 1, :, piece_of(p)],
-            ring_in.at[step - 1, :, piece_of(p)],
-            ring_send.at[step - 1],
-            ring_recv.at[step - 1, p],
+        for part, steps in enumerate((ORDER[:1], ORDER[1:])):
+
+            def body(p, carry, part=part, steps=steps):
+                for step in steps:
+                    pair_out[ORDER.index(step), :, piece_of(p)] = weighted(
+                        shares[step], 1 - core, step, piece_of(p)
+                    )
+                pair_copy(part, p).start()
+                return carry
+
+            lax.fori_loop(0, pieces, body, 0)
+
+    def hop(slot, p, odd=0):
+        step = (1 - 2 * odd, 1, -1)[slot]
+        peer = group_of(step + ring, core)
+        codes = remote(
+            ring_out.at[slot, :, piece_of(p)],
+            ring_in.at[slot, :, piece_of(p)],
+            ring_send.at[slot],
+            ring_recv.at[slot, p],
             "ep",
-            group_of(step, core),
-        )
+            peer,
+        )
+        scale = remote(
+            scale_out.at[slot, p],
+            scale_in.at[slot, p],
+            scale_send.at[slot],
+            ring_recv.at[slot, p],
+            "ep",
+            peer,
+        )
+        return codes, scale
+
+    def landed(slot, p):
+        remote(tally, tally, ring_send.at[slot], ring_recv.at[slot, p], "ep", partner).wait_recv()
+
+    def spread_lanes(row, width):
+        return jnp.concatenate([row] * (width // LANES), axis=1)
+
+    def pair_sum(step, cols):
+        total = weighted(shares[step], core, step, cols).astype(jnp.float32)
+        return total + pair_in[ORDER.index(step), :, cols].astype(jnp.float32)
+
+    def decode(slot, p, cols, width):
+        codes = ring_in[slot, :, cols].astype(jnp.int32).astype(jnp.float32)
+        return codes * spread_lanes(scale_in[slot, p], width)
+
+    def encode(slot, p, odd, total):
+        most = jnp.max(jnp.abs(total), axis=0, keepdims=True)
+        parts = [most[:, j : j + LANES] for j in range(0, piece, LANES)]
+        most = jnp.maximum(functools.reduce(jnp.maximum, parts), TINY)
+        scale_out[slot, p] = most * (1.0 / CODES)
+        codes = lax.round(
+            total * spread_lanes(CODES / most, piece), lax.RoundingMethod.TO_NEAREST_EVEN
+        )
+        ring_out[slot, :, piece_of(p)] = codes.astype(jnp.int32).astype(jnp.int16)
+        for copy in hop(slot, p, odd):
+            copy.start()
 
     @pl.when(core != FIRST)
     def _():
@@ -230,44 +260,48 @@
         pl.semaphore_wait(gate, 1)
 
     shares = [share_of(group_of(step, core)) for step in range(ring)]
-    order = sorted(range(1, ring), key=lambda step: abs(2 * step - ring))
-
-    def scale_copy(step, p):
-        return remote(
-            scale_out.at[step - 1, p],
-            scale_in.at[step - 1, p],
-            scale_send.at[step - 1],
-            scale_recv.at[step - 1, p],
-            "ep",
-            group_of(step, core),
-        )
-
-    def spread_lanes(row, width):
-        return jnp.concatenate([row] * (width // LANES), axis=1)
-
-    def send_piece(p, carry):
-        pair_copy(p).wait_recv()
-        cols = piece_of(p)
-        for step in order:
-            total = weighted(shares[step], core, step, cols).astype(jnp.float32)
-            total = total + pair_in[step, :, cols].astype(jnp.float32)
-            most = jnp.max(jnp.abs(total), axis=0, keepdims=True)
-            parts = [most[:, j : j + LANES] for j in range(0, piece, LANES)]
-            most = jnp.maximum(functools.reduce(jnp.maximum, parts), TINY)
-            scale_out[step - 1, p] = most * (1.0 / CODES)
-            codes = lax.round(
-                total * spread_lanes(CODES / most, piece), lax.RoundingMethod.TO_NEAREST_EVEN
-            )
-            ring_out[step - 1, :, cols] = codes.astype(jnp.int32).astype(jnp.int16)
-            ring_copy(step, p).start()
-            scale_copy(step, p).start()
+    @pl.when(core != FIRST)
+    def _():
+        slabs_in(1 - FIRST)
+
+    def far(q, carry):
+        for odd in range(2):
+            p = 2 * q + odd
+            pair_copy(0, p).wait_recv()
+            encode(0, p, odd, pair_sum(2, piece_of(p)))
         return carry
 
-    lax.fori_loop(0, pieces, send_piece, 0)
+    lax.fori_loop(0, pieces // 2, far, 0)
+
+    def near(q, carry):
+        for odd in range(2):
+            p = 2 * q + odd
+            pair_copy(1, p).wait_recv()
+            slot, step = ((2, 3), (1, 1))[odd]
+            encode(slot, p, odd, pair_sum(step, piece_of(p)))
+            slot, step = ((1, 1), (2, 3))[odd]
+            landed(0, p)
+            encode(slot, p, odd, pair_sum(step, piece_of(p)) + decode(0, p, piece_of(p), piece))
+        return carry
+
+    lax.fori_loop(0, pieces // 2, near, 0)
 
     @pl.when(core == FIRST)
     def _():
+        slabs_in(1 - FIRST)
         give()
+
+    for copy in small[1:]:
+        copy.wait()
+    params = [
+        pltpu.make_async_copy(src.at[0], dst, param_sem.at[i])
+        for i, (src, dst) in enumerate(
+            ((mom_hbm, mom), (second_hbm, second), (weight_hbm, weight))
+        )
+    ]
+    for copy in params:
+        copy.start()
+
 
     shape = (rows, layer.shape[1])
     lane = lax.broadcasted_iota(jnp.int32, shape, 1)
@@ -295,12 +329,8 @@
         copy.wait()
 
     def moments(p, carry):
-        for step in range(1, ring):
-            ring_copy(step, p).wait_recv()
-            scale_copy(step, p).wait_recv()
-        scales = [
-            spread_lanes(scale_in[step - 1, p], narrow) for step in range(1, ring)
-        ]
+        for slot in (1, 2):
+            landed(slot, p)
 
         @pl.when(jnp.logical_and(core == FIRST, p == GATE_PIECE))
         def _():
@@ -314,11 +344,7 @@
         def one(i, inner):
             grad_acc, mom_acc = inner
             cols = cols_of(p, i)
-            total = weighted(shares[0], core, 0, cols).astype(jnp.float32)
-            total = total + pair_in[0, :, cols].astype(jnp.float32)
-            for step in range(1, ring):
-                codes = ring_in[step - 1, :, cols].astype(jnp.int32).astype(jnp.float32)
-                total = total + codes * scales[step - 1]
+            total = pair_sum(0, cols) + decode(1, p, cols, narrow) + decode(2, p, cols, narrow)
             mom_next = MOMENTUM_DECAY * mom[:, cols] + (1.0 - MOMENTUM_DECAY) * total
             gradient[:, cols] = total
             mom[:, cols] = mom_next
@@ -327,7 +353,7 @@
             )
             return grad_acc + total * total, mom_acc + mom_next * mom_next
 
-        return lax.fori_loop(0, piece // narrow, one, carry)
+        return lax.fori_loop(0, piece // narrow, one, carry, unroll=True)
 
     zero = jnp.zeros((rows, narrow), jnp.float32)
     grad_acc, mom_acc = lax.fori_loop(0, pieces, moments, (zero, zero))
@@ -425,49 +451,45 @@
     def send(source, k, role, recv, peer):
         remote(block(source, k), block(source, k), row_send.at[role], recv, "fs", peer).start()
 
-    def spread(source, k, role, part, at, way):
-        send(source, k, role, pass_recv.at[part, k], at(0, way))
+    def spread(source, k, role, at, way):
+        send(source, k, role, pass_recv.at[role, k], at(0, way))
         send(source, k, role, last_recv.at[source], at(0, -way))
 
-    def arrive(source, k, part):
-        remote(
-            block(source, k), block(source, k), row_send.at[0], pass_recv.at[part, k], "fs", source
-        ).wait_recv()
+    def arrive(stage, k, count):
+        part = gathered.at[pl.ds(0, count * rows), pl.ds(pl.multiple_of(k * width, width), width)]
+        remote(part, part, row_send.at[0], pass_recv.at[stage, k], "fs", me).wait_recv()
+
+    def pass_on(k, role, first):
+        at, turn = route(k)
+        way = turn if first % 2 == 0 else -turn
+        source = at(first * turn, -way)
+        send(source, k, role, last_recv.at[source], at(0, way))
 
     def own(k):
         at, turn = route(k)
         send(me, k, 0, pass_recv.at[0, k], at(turn, 0))
-        send(me, k, 0, pass_recv.at[1, k], at(-turn, 0))
-        spread(me, k, 0, 3, at, turn)
-
-    def pass_on(k, role, first, part):
-        at, turn = route(k)
-        way = turn if first % 2 == 0 else -turn
-        source = at(first * turn, -way)
-        arrive(source, k, part)
-        send(source, k, role, last_recv.at[source], at(0, way))
+        send(me, k, 0, pass_recv.at[0, k], at(-turn, 0))
+        spread(me, k, 0, at, turn)
 
     def relay_one(k):
         at, turn = route(k)
+        arrive(0, k, 3)
         source = at(-turn, 0)
-        arrive(source, k, 0)
-        send(source, k, 1, pass_recv.at[2, k], at(turn, 0))
-        spread(source, k, 1, 4, at, -turn)
-        source = at(turn, 0)
-        arrive(source, k, 1)
-        spread(source, k, 1, 5, at, -turn)
-        pass_on(k, 1, 0, 3)
+        send(source, k, 1, pass_recv.at[1, k], at(turn, 0))
+        spread(source, k, 1, at, -turn)
+        spread(at(turn, 0), k, 1, at, -turn)
+        pass_on(k, 1, 0)
 
     def relay_two(k):
         at, turn = route(k)
-        source = at(2, 0)
-        arrive(source, k, 2)
-        spread(source, k, 2, 6, at, turn)
-        pass_on(k, 2, -1, 4)
-        pass_on(k, 2, 1, 5)
+        arrive(1, k, 3)
+        spread(at(2, 0), k, 2, at, turn)
+        pass_on(k, 2, -1)
+        pass_on(k, 2, 1)
 
     def relay_three(k):
-        pass_on(k, 3, 2, 6)
+        arrive(2, k, 1)
+        pass_on(k, 3, 2)
 
     def turn_of(t, carry):
         for lag, relay in ((LAG_ONE, relay_one), (LAG_TWO, relay_two), (LAG_THREE, relay_three)):
@@ -491,23 +513,17 @@
 
     lax.fori_loop(0, chunks + LAG_THREE, turn_of, 0)
 
-    remote(pair_out, pair_in, pair_send, pair_recv.at[0], "ep", partner).wait_send()
-    for step in range(1, ring):
+    for part in range(2):
+        slots = (pl.ds(0, 1), pl.ds(1, ring - 1))[part]
         remote(
-            ring_out.at[step - 1],
-            ring_in.at[step - 1],
-            ring_send.at[step - 1],
-            ring_recv.at[step - 1, 0],
-            "ep",
-            group_of(step, core),
+            pair_out.at[slots], pair_in.at[slots], pair_send.at[part], pair_recv.at[part, 0], "ep", partner
+        ).wait_send()
+    for slot in range(3):
+        remote(
+            ring_out.at[slot], ring_in.at[slot], ring_send.at[slot], ring_recv.at[slot, 0], "ep", partner
         ).wait_send()
         remote(
-            scale_out.at[step - 1],
-            scale_in.at[step - 1],
-            scale_send.at[step - 1],
-            scale_recv.at[step - 1, 0],
-            "ep",
-            group_of(step, core),
+            scale_out.at[slot], scale_in.at[slot], scale_send.at[slot], ring_recv.at[slot, 0], "ep", partner
         ).wait_send()
     all_sums.wait_send()
     share = {0: 0, 1: chunks // 4, 2: chunks // 2, 3: chunks // 4}
@@ -578,20 +594,20 @@
             pltpu.VMEM((rows, columns), jnp.float32),
             pltpu.VMEM((shards, 2, LANES), jnp.float32),
             pltpu.VMEM((in_bias.shape[0] * rows, 16 * rows), jnp.bfloat16),
+            pltpu.VMEM((rows * columns // pieces * 2 // (4 * LANES) + 1, LANES), jnp.float32),
             pltpu.SemaphoreType.DMA((5,)),
-            pltpu.SemaphoreType.DMA((CORES, ring)),
+            pltpu.SemaphoreType.DMA((CORES,)),
             pltpu.SemaphoreType.DMA((3,)),
-            pltpu.SemaphoreType.DMA,
-            pltpu.SemaphoreType.DMA((pieces,)),
+            pltpu.SemaphoreType.DMA((2,)),
+            pltpu.SemaphoreType.DMA((2, pieces)),
             pltpu.SemaphoreType.DMA((ring - 1,)),
             pltpu.SemaphoreType.DMA((ring - 1, pieces)),
             pltpu.SemaphoreType.DMA((ring - 1,)),
-            pltpu.SemaphoreType.DMA((ring - 1, pieces)),
             pltpu.SemaphoreType.REGULAR,
             pltpu.SemaphoreType.DMA,
             pltpu.SemaphoreType.DMA,
             pltpu.SemaphoreType.DMA((4,)),
-            pltpu.SemaphoreType.DMA((7, chunks)),
+            pltpu.SemaphoreType.DMA((3, chunks)),
             pltpu.SemaphoreType.DMA((shards,)),
         ],
         compiler_params=pltpu.CompilerParams(

time: 76.6 us -> 73.2 us (0.956)
  Pallas kernels: 75.9 us -> 72.4 us
    pallas_call x1, Pallas kernels: 72.2 us -> 68.8 us  [per_device(): pl.pallas_call(functools.partial(kernel, ring), out_shape=(pltpu.VMEM((1,...]
where the time goes in v3:
time: 73.2 us; the launch traced here: 73.1 us
  Pallas kernels  72.4 us (99%)
    pallas_call x1, Pallas kernels, per_device(): pl.pallas_call(functools.partial(kernel, ring), out_shape=(pltpu.VMEM((1,...  68.8 us
    pallas_call x1, Pallas kernels, per_device(): pl.pallas_call(store, out_shape=[jax.ShapeDtypeStruct(r.shape, r.dtype) f...  3.62 us

profile of v3, /device:TPU:0, one launch (start us, length us, event | category | flops | bytes accessed | tf_op | source)
XLA Modules:
  0.0 73.1 jit_solution(86046597679314)
XLA Ops:
  0.6 68.8 %learned_update.1 = (bf16[1,256,14336]{2,1,0:T(8,128)(2,1)S(1)}, f32[1,16,14336]{2,1,0:T(8,128)S(1)}, f32[1,16,14336]{2,1,0:T(8,128)S(1)}) custom-call(s32[8,8]{1,0:T(8,128)} %counts_hbm.1, f32[6,32]{1,0:T(8,128)} %in_weight_hbm.1, f32[32]{0:T(128)} %in_bias_hbm.1, f32[2,32]{1,0:T(2,128)} %bitcast.1, f32[2]{0:T(128)} %out_bias_hbm.1, ...), custom_call_target="tpu_custom_call" | custom-call | tf_op jit(solution)/shard_map/learned_update/pallas_call | solution.py:571
  69.5 3.6 %store_results.1 = (bf16[1,256,14336]{2,1,0:T(8,128)(2,1)}, f32[1,16,14336]{2,1,0:T(8,128)}, f32[1,16,14336]{2,1,0:T(8,128)}) custom-call(bf16[1,256,14336]{2,1,0:T(8,128)(2,1)S(1)} %get-tuple-element.6.gathered, f32[1,16,14336]{2,1,0:T(8,128)S(1)} %get-tuple-element.7.mom, f32[1,16,14336]{2,1,0:T(8,128)S(1)} %get-tuple-element.8.second), custom_call_target="tpu_custom_call" | custom-call | tf_op jit(solution)/shard_map/store_results/pallas_call | solution.py:618

commit v4 on v3

--- a/solution.py
+++ b/solution.py
@@ -90,6 +90,7 @@
     ring_recv,
     scale_send,
     gate,
+    ready,
     sum_send,
     sum_recv,
     row_send,
@@ -145,17 +146,24 @@
         for step in ORDER:
             slab(which, step).start()
     barrier = pltpu.get_barrier_semaphore()
-    for peer in [partner] + [group_of(step, core) for step in range(1, ring)]:
-        pl.semaphore_signal(
-            barrier, inc=1, device_id={"ep": peer}, device_id_type=pl.DeviceIdType.MESH
-        )
-    for step in range(1, shards):
-        pl.semaphore_signal(
-            barrier,
-            inc=1,
-            device_id={"fs": (me + step) % shards},
-            device_id_type=pl.DeviceIdType.MESH,
-        )
+    near = [
+        {"fs": up * SIDE + along}
+        for up, along in (
+            (z, (x + 1) % SIDE),
+            (z, (x + SIDE - 1) % SIDE),
+            ((z + 1) % SIDE, x),
+            ((z + SIDE - 1) % SIDE, x),
+        )
+    ]
+
+    def greet(semaphore, peers):
+        for peer in peers:
+            pl.semaphore_signal(
+                semaphore, inc=1, device_id=peer, device_id_type=pl.DeviceIdType.MESH
+            )
+
+    beside = [{"ep": peer} for peer in (partner, group_of(1, core), group_of(ring - 1, core))]
+    greet(barrier, beside + near)
     small[0].wait()
 
     pieces = ring_recv.shape[1]
@@ -180,7 +188,8 @@
         return value.astype(jnp.bfloat16)
 
     slabs_in(FIRST)
-    pl.semaphore_wait(barrier, 1 + ring - 1 + shards - 1)
+    pl.semaphore_wait(barrier, len(beside) + len(near))
+    greet(ready.at[0], near)
 
     def pair_copy(part, p):
         slots = (pl.ds(0, 1), pl.ds(1, ring - 1))[part]
@@ -273,7 +282,7 @@
 
     lax.fori_loop(0, pieces // 2, far, 0)
 
-    def near(q, carry):
+    def combine(q, carry):
         for odd in range(2):
             p = 2 * q + odd
             pair_copy(1, p).wait_recv()
@@ -284,8 +293,10 @@
             encode(slot, p, odd, pair_sum(step, piece_of(p)) + decode(0, p, piece_of(p), piece))
         return carry
 
-    lax.fori_loop(0, pieces // 2, near, 0)
-
+    lax.fori_loop(0, pieces // 2, combine, 0)
+
+    pl.semaphore_wait(ready.at[0], len(near))
+    greet(ready.at[1], near)
     @pl.when(core == FIRST)
     def _():
         slabs_in(1 - FIRST)
@@ -325,6 +336,8 @@
         return carry
 
     lax.fori_loop(0, units, place, 0)
+    pl.semaphore_wait(ready.at[1], len(near))
+    greet(ready.at[2], near)
     for copy in params:
         copy.wait()
 
@@ -362,6 +375,7 @@
         acc = jnp.sum(acc, axis=0, keepdims=True)
         return sum(acc[:, j : j + LANES] for j in range(0, narrow, LANES))
 
+    pl.semaphore_wait(ready.at[2], len(near))
     sums[me, 0:1, :] = to_lanes(grad_acc)
     sums[me, 1:2, :] = to_lanes(mom_acc)
     for step in range(1, shards):
@@ -604,6 +618,7 @@
             pltpu.SemaphoreType.DMA((ring - 1, pieces)),
             pltpu.SemaphoreType.DMA((ring - 1,)),
             pltpu.SemaphoreType.REGULAR,
+            pltpu.SemaphoreType.REGULAR((3,)),
             pltpu.SemaphoreType.DMA,
             pltpu.SemaphoreType.DMA,
             pltpu.SemaphoreType.DMA((4,)),

time: 73.2 us -> 71.5 us (0.977)
  Pallas kernels: 72.4 us -> 70.8 us
    pallas_call x1, Pallas kernels: 68.8 us -> 67.2 us  [per_device(): pl.pallas_call(functools.partial(kernel, ring), out_shape=(pltpu.VMEM((1,...]
where the time goes in v4:
time: 71.5 us; the launch traced here: 71.4 us
  Pallas kernels  70.8 us (99%)
    pallas_call x1, Pallas kernels, per_device(): pl.pallas_call(functools.partial(kernel, ring), out_shape=(pltpu.VMEM((1,...  67.2 us
    pallas_call x1, Pallas kernels, per_device(): pl.pallas_call(store, out_shape=[jax.ShapeDtypeStruct(r.shape, r.dtype) f...  3.62 us

profile of v4, /device:TPU:0, one launch (start us, length us, event | category | flops | bytes accessed | tf_op | source)
XLA Modules:
  0.0 71.4 jit_solution(17370445935772582779)
XLA Ops:
  0.6 67.2 %learned_update.1 = (bf16[1,256,14336]{2,1,0:T(8,128)(2,1)S(1)}, f32[1,16,14336]{2,1,0:T(8,128)S(1)}, f32[1,16,14336]{2,1,0:T(8,128)S(1)}) custom-call(s32[8,8]{1,0:T(8,128)} %counts_hbm.1, f32[6,32]{1,0:T(8,128)} %in_weight_hbm.1, f32[32]{0:T(128)} %in_bias_hbm.1, f32[2,32]{1,0:T(2,128)} %bitcast.1, f32[2]{0:T(128)} %out_bias_hbm.1, ...), custom_call_target="tpu_custom_call" | custom-call | tf_op jit(solution)/shard_map/learned_update/pallas_call | solution.py:585
  67.8 3.6 %store_results.1 = (bf16[1,256,14336]{2,1,0:T(8,128)(2,1)}, f32[1,16,14336]{2,1,0:T(8,128)}, f32[1,16,14336]{2,1,0:T(8,128)}) custom-call(bf16[1,256,14336]{2,1,0:T(8,128)(2,1)S(1)} %get-tuple-element.6.gathered, f32[1,16,14336]{2,1,0:T(8,128)S(1)} %get-tuple-element.7.mom, f32[1,16,14336]{2,1,0:T(8,128)S(1)} %get-tuple-element.8.second), custom_call_target="tpu_custom_call" | custom-call | tf_op jit(solution)/shard_map/store_results/pallas_call | solution.py:633

commit v5 on v4

--- a/solution.py
+++ b/solution.py
@@ -392,27 +392,28 @@
         totals = totals + sums[s]
     mean = jnp.broadcast_to(jnp.sum(totals, axis=1, keepdims=True) / entries, (2, LANES)) + NORM_EPS
     inverse = lax.rsqrt(mean)
-    inv_grad = inverse[0:1, :1]
-    inv_mom = inverse[1:2, :1]
-    log_mom = jnp.max(0.5 * jnp.log(mean[1:2, :]))
+    log_mom = 0.5 * jnp.log(mean[1:2, :])
     tail = pl.ds(shape[1] - LANES, LANES)
     biased = slot[:, -LANES:] >= 14
     first = slot[:, -LANES:] == 14
     ends = diagonal[:, -LANES:]
 
     def settle(h, carry):
-        high, low = halves(jnp.full(ends.shape, in_bias[h] + in_weight[5, h] * log_mom))
+        value = in_bias[h] + in_weight[5, h] * log_mom
+        high, low = halves(jnp.broadcast_to(value, ends.shape))
         span = pl.ds(pl.multiple_of(h * rows, rows), rows)
         block = jnp.where(ends, jnp.where(first, high, low), 0.0)
         kept = layer[span, tail].astype(jnp.float32)
         layer[span, tail] = jnp.where(biased, block, kept).astype(jnp.bfloat16)
         return carry
 
-    lax.fori_loop(0, units, settle, 0)
+    lax.fori_loop(0, units, settle, 0, unroll=True)
 
     chunks = pass_recv.shape[1]
     width = columns // chunks
     tile = tile_width(width, TILE)
+    inv_grad = spread_lanes(inverse[0:1, :], tile)
+    inv_mom = spread_lanes(inverse[1:2, :], tile)
 
     def learned_step(cols):
         grad = gradient[:, cols]
@@ -467,7 +468,7 @@
 
     def spread(source, k, role, at, way):
         send(source, k, role, pass_recv.at[role, k], at(0, way))
-        send(source, k, role, last_recv.at[source], at(0, -way))
+        send(source, k, role, last_recv, at(0, -way))
 
     def arrive(stage, k, count):
         part = gathered.at[pl.ds(0, count * rows), pl.ds(pl.multiple_of(k * width, width), width)]
@@ -477,7 +478,7 @@
         at, turn = route(k)
         way = turn if first % 2 == 0 else -turn
         source = at(first * turn, -way)
-        send(source, k, role, last_recv.at[source], at(0, way))
+        send(source, k, role, last_recv, at(0, way))
 
     def own(k):
         at, turn = route(k)
@@ -540,19 +541,12 @@
             scale_out.at[slot], scale_in.at[slot], scale_send.at[slot], ring_recv.at[slot, 0], "ep", partner
         ).wait_send()
     all_sums.wait_send()
-    share = {0: 0, 1: chunks // 4, 2: chunks // 2, 3: chunks // 4}
-    for up in range(SIDE):
-        for along in range(SIDE):
-            number = share[up] + share[along]
-            if number == 0:
-                continue
-            source = (z + up) % SIDE * SIDE + (x + along) % SIDE
-            part = gathered.at[rows_of(source), pl.ds(0, number * width)]
-            remote(part, part, row_send.at[0], last_recv.at[source], "fs", source).wait_recv()
+    part = gathered.at[pl.ds(0, 8 * rows), :]
+    remote(part, part, row_send.at[0], last_recv, "fs", me).wait_recv()
     for role, number in enumerate((4, 6, 4, 1)):
         part = gathered.at[pl.ds(0, number * rows), :]
         remote(
-            part, part, row_send.at[role], last_recv.at[me], "fs", (me + 1) % shards
+            part, part, row_send.at[role], last_recv, "fs", (me + 1) % shards
         ).wait_send()
 
 
@@ -623,7 +617,7 @@
             pltpu.SemaphoreType.DMA,
             pltpu.SemaphoreType.DMA((4,)),
             pltpu.SemaphoreType.DMA((3, chunks)),
-            pltpu.SemaphoreType.DMA((shards,)),
+            pltpu.SemaphoreType.DMA,
         ],
         compiler_params=pltpu.CompilerParams(
             collective_id=0, has_side_effects=True, vmem_limit_bytes=VMEM_BYTES

time: 71.5 us -> 71 us (level)
  no operation moved by 1% of the time
where the time goes in v5:
time: 71 us; the launch traced here: 70.9 us
  Pallas kernels  70.2 us (99%)
    pallas_call x1, Pallas kernels, per_device(): pl.pallas_call(functools.partial(kernel, ring), out_shape=(pltpu.VMEM((1,...  66.6 us
    pallas_call x1, Pallas kernels, per_device(): pl.pallas_call(store, out_shape=[jax.ShapeDtypeStruct(r.shape, r.dtype) f...  3.62 us

profile of v5, /device:TPU:0, one launch (start us, length us, event | category | flops | bytes accessed | tf_op | source)
XLA Modules:
  0.0 70.9 jit_solution(1360002708323065880)
XLA Ops:
  0.6 66.6 %learned_update.1 = (bf16[1,256,14336]{2,1,0:T(8,128)(2,1)S(1)}, f32[1,16,14336]{2,1,0:T(8,128)S(1)}, f32[1,16,14336]{2,1,0:T(8,128)S(1)}) custom-call(s32[8,8]{1,0:T(8,128)} %counts_hbm.1, f32[6,32]{1,0:T(8,128)} %in_weight_hbm.1, f32[32]{0:T(128)} %in_bias_hbm.1, f32[2,32]{1,0:T(2,128)} %bitcast.1, f32[2]{0:T(128)} %out_bias_hbm.1, ...), custom_call_target="tpu_custom_call" | custom-call | tf_op jit(solution)/shard_map/learned_update/pallas_call | solution.py:579
  67.3 3.6 %store_results.1 = (bf16[1,256,14336]{2,1,0:T(8,128)(2,1)}, f32[1,16,14336]{2,1,0:T(8,128)}, f32[1,16,14336]{2,1,0:T(8,128)}) custom-call(bf16[1,256,14336]{2,1,0:T(8,128)(2,1)S(1)} %get-tuple-element.6.gathered, f32[1,16,14336]{2,1,0:T(8,128)S(1)} %get-tuple-element.7.mom, f32[1,16,14336]{2,1,0:T(8,128)S(1)} %get-tuple-element.8.second), custom_call_target="tpu_custom_call" | custom-call | tf_op jit(solution)/shard_map/store_results/pallas_call | solution.py:627

commit v6 on v5

--- a/solution.py
+++ b/solution.py
@@ -378,10 +378,16 @@
     pl.semaphore_wait(ready.at[2], len(near))
     sums[me, 0:1, :] = to_lanes(grad_acc)
     sums[me, 1:2, :] = to_lanes(mom_acc)
-    for step in range(1, shards):
-        remote(
-            sums.at[me], sums.at[me], sum_send, sum_recv, "fs", (me + step) % shards
-        ).start()
+    def hops(offset):
+        return min(offset, SIDE - offset)
+
+    offsets = sorted(
+        ((up, along) for up in range(SIDE) for along in range(SIDE)),
+        key=lambda pair: -hops(pair[0]) - hops(pair[1]),
+    )
+    for up, along in offsets[:-1]:
+        peer = (z + up) % SIDE * SIDE + (x + along) % SIDE
+        remote(sums.at[me], sums.at[me], sum_send, sum_recv, "fs", peer).start()
     others = sums.at[pl.ds(0, shards - 1)]
     all_sums = remote(others, others, sum_send, sum_recv, "fs", (me + 1) % shards)
     all_sums.wait_recv()

time: 71 us -> 71 us (level)
  no operation moved by 1% of the time
where the time goes in v6:
time: 71 us; the launch traced here: 70.8 us
  Pallas kernels  70.2 us (99%)
    pallas_call x1, Pallas kernels, per_device(): pl.pallas_call(functools.partial(kernel, ring), out_shape=(pltpu.VMEM((1,...  66.5 us
    pallas_call x1, Pallas kernels, per_device(): pl.pallas_call(store, out_shape=[jax.ShapeDtypeStruct(r.shape, r.dtype) f...  3.62 us

profile of v6, /device:TPU:0, one launch (start us, length us, event | category | flops | bytes accessed | tf_op | source)
XLA Modules:
  0.0 70.8 jit_solution(6696700786262999279)
XLA Ops:
  0.6 66.5 %learned_update.1 = (bf16[1,256,14336]{2,1,0:T(8,128)(2,1)S(1)}, f32[1,16,14336]{2,1,0:T(8,128)S(1)}, f32[1,16,14336]{2,1,0:T(8,128)S(1)}) custom-call(s32[8,8]{1,0:T(8,128)} %counts_hbm.1, f32[6,32]{1,0:T(8,128)} %in_weight_hbm.1, f32[32]{0:T(128)} %in_bias_hbm.1, f32[2,32]{1,0:T(2,128)} %bitcast.1, f32[2]{0:T(128)} %out_bias_hbm.1, ...), custom_call_target="tpu_custom_call" | custom-call | tf_op jit(solution)/shard_map/learned_update/pallas_call | solution.py:585
  67.2 3.6 %store_results.1 = (bf16[1,256,14336]{2,1,0:T(8,128)(2,1)}, f32[1,16,14336]{2,1,0:T(8,128)}, f32[1,16,14336]{2,1,0:T(8,128)}) custom-call(bf16[1,256,14336]{2,1,0:T(8,128)(2,1)S(1)} %get-tuple-element.6.gathered, f32[1,16,14336]{2,1,0:T(8,128)S(1)} %get-tuple-element.7.mom, f32[1,16,14336]{2,1,0:T(8,128)S(1)} %get-tuple-element.8.second), custom_call_target="tpu_custom_call" | custom-call | tf_op jit(solution)/shard_map/store_results/pallas_call | solution.py:633

commit v7 on v6

--- a/solution.py
+++ b/solution.py
@@ -22,6 +22,7 @@
 LAG_TWO = 11
 LAG_THREE = 16
 GATE_PIECE = 6
+EARLY = 3
 FIRST = 1
 ORDER = (2, 1, 3, 0)
 CODES = 32767.0
@@ -514,9 +515,10 @@
 
     def turn_of(t, carry):
         for lag, relay in ((LAG_ONE, relay_one), (LAG_TWO, relay_two), (LAG_THREE, relay_three)):
-            k = t - lag
-
-            @pl.when(jnp.logical_and(k >= 0, k < chunks))
+            early = t - lag + 1 < EARLY
+            k = t - lag + jnp.where(early, 1, 0)
+
+            @pl.when(jnp.logical_and(k >= jnp.where(early, 0, EARLY), k < chunks))
             def _(k=k, relay=relay):
                 relay(k)
 

time: 71 us -> 71.1 us (level)
  no operation moved by 1% of the time
where the time goes in v7:
time: 71.1 us; the launch traced here: 71 us
  Pallas kernels  70.4 us (99%)
    pallas_call x1, Pallas kernels, per_device(): pl.pallas_call(functools.partial(kernel, ring), out_shape=(pltpu.VMEM((1,...  66.8 us
    pallas_call x1, Pallas kernels, per_device(): pl.pallas_call(store, out_shape=[jax.ShapeDtypeStruct(r.shape, r.dtype) f...  3.62 us

profile of v7, /device:TPU:0, one launch (start us, length us, event | category | flops | bytes accessed | tf_op | source)
XLA Modules:
  0.0 71.0 jit_solution(12082126437821172190)
XLA Ops:
  0.6 66.8 %learned_update.1 = (bf16[1,256,14336]{2,1,0:T(8,128)(2,1)S(1)}, f32[1,16,14336]{2,1,0:T(8,128)S(1)}, f32[1,16,14336]{2,1,0:T(8,128)S(1)}) custom-call(s32[8,8]{1,0:T(8,128)} %counts_hbm.1, f32[6,32]{1,0:T(8,128)} %in_weight_hbm.1, f32[32]{0:T(128)} %in_bias_hbm.1, f32[2,32]{1,0:T(2,128)} %bitcast.1, f32[2]{0:T(128)} %out_bias_hbm.1, ...), custom_call_target="tpu_custom_call" | custom-call | tf_op jit(solution)/shard_map/learned_update/pallas_call | solution.py:587
  67.4 3.6 %store_results.1 = (bf16[1,256,14336]{2,1,0:T(8,128)(2,1)}, f32[1,16,14336]{2,1,0:T(8,128)}, f32[1,16,14336]{2,1,0:T(8,128)}) custom-call(bf16[1,256,14336]{2,1,0:T(8,128)(2,1)S(1)} %get-tuple-element.6.gathered, f32[1,16,14336]{2,1,0:T(8,128)S(1)} %get-tuple-element.7.mom, f32[1,16,14336]{2,1,0:T(8,128)S(1)} %get-tuple-element.8.second), custom_call_target="tpu_custom_call" | custom-call | tf_op jit(solution)/shard_map/store_results/pallas_call | solution.py:635

commit v8 on v6

--- a/solution.py
+++ b/solution.py
@@ -183,6 +183,9 @@
         mine = jnp.full((1, LANES), counts[me_group, expert].astype(jnp.float32))
         return (mine / jnp.full((1, LANES), total.astype(jnp.float32)))[:, :1]
 
+    gift_shares = [share_of(group_of(step, 1 - core)) for step in range(ring)]
+    shares = [share_of(group_of(step, core)) for step in range(ring)]
+
     def weighted(share, which, step, cols):
         value = share * grads[which, step, :, cols].astype(jnp.float32)
         return value.astype(jnp.bfloat16)
@@ -203,13 +206,12 @@
         )
 
     def give():
-        shares = [share_of(group_of(step, 1 - core)) for step in range(ring)]
         for part, steps in enumerate((ORDER[:1], ORDER[1:])):
 
             def body(p, carry, part=part, steps=steps):
                 for step in steps:
                     pair_out[ORDER.index(step), :, piece_of(p)] = weighted(
-                        shares[step], 1 - core, step, piece_of(p)
+                        gift_shares[step], 1 - core, step, piece_of(p)
                     )
                 pair_copy(part, p).start()
                 return carry
@@ -268,7 +270,6 @@
         give()
         pl.semaphore_wait(gate, 1)
 
-    shares = [share_of(group_of(step, core)) for step in range(ring)]
     @pl.when(core != FIRST)
     def _():
         slabs_in(1 - FIRST)

time: 71 us -> 70.9 us (level)
  no operation moved by 1% of the time
where the time goes in v8:
time: 70.9 us; the launch traced here: 70.8 us
  Pallas kernels  70.1 us (99%)
    pallas_call x1, Pallas kernels, per_device(): pl.pallas_call(functools.partial(kernel, ring), out_shape=(pltpu.VMEM((1,...  66.5 us
    pallas_call x1, Pallas kernels, per_device(): pl.pallas_call(store, out_shape=[jax.ShapeDtypeStruct(r.shape, r.dtype) f...  3.62 us

profile of v8, /device:TPU:0, one launch (start us, length us, event | category | flops | bytes accessed | tf_op | source)
XLA Modules:
  0.0 70.8 jit_solution(13109517393179793347)
XLA Ops:
  0.6 66.5 %learned_update.1 = (bf16[1,256,14336]{2,1,0:T(8,128)(2,1)S(1)}, f32[1,16,14336]{2,1,0:T(8,128)S(1)}, f32[1,16,14336]{2,1,0:T(8,128)S(1)}) custom-call(s32[8,8]{1,0:T(8,128)} %counts_hbm.1, f32[6,32]{1,0:T(8,128)} %in_weight_hbm.1, f32[32]{0:T(128)} %in_bias_hbm.1, f32[2,32]{1,0:T(2,128)} %bitcast.1, f32[2]{0:T(128)} %out_bias_hbm.1, ...), custom_call_target="tpu_custom_call" | custom-call | tf_op jit(solution)/shard_map/learned_update/pallas_call | solution.py:586
  67.2 3.6 %store_results.1 = (bf16[1,256,14336]{2,1,0:T(8,128)(2,1)}, f32[1,16,14336]{2,1,0:T(8,128)}, f32[1,16,14336]{2,1,0:T(8,128)}) custom-call(bf16[1,256,14336]{2,1,0:T(8,128)(2,1)S(1)} %get-tuple-element.6.gathered, f32[1,16,14336]{2,1,0:T(8,128)S(1)} %get-tuple-element.7.mom, f32[1,16,14336]{2,1,0:T(8,128)S(1)} %get-tuple-element.8.second), custom_call_target="tpu_custom_call" | custom-call | tf_op jit(solution)/shard_map/store_results/pallas_call | solution.py:634
